TPU v7x, 256 devices: a whole 4x4x8 slice. The times are simulated.
256 devices in a mesh: panel: 64 (over z, x, core), obs: 4 (over y).
Axes of the slice: x: 4, y: 4, z: 8, core: 2. Of those that a mesh axis runs over, the one named last changes fastest.
Arguments:
- samples: bfloat16 [1024, 4, 32768], P(('panel', 'obs')), may hold values from -6 to 6
- panel_position: float32 [3, 32768], P(None, 'panel'), may hold values from -1 to 1
- panel_area: float32 [32768], P('panel'), may hold values from 0.5 to 2
- panel_counts: int32 [256], P('panel'), may hold values from 1 to 128
- obs_position: float32 [3, 1024], P(None, 'obs'), may hold values from -12 to 12, as said below
- freq_bins: int32 [32], replicated, may hold values from 1 to 511
Outputs:
- far_pressure: float32 [2, 32, 1024], P(None, None, ('obs', 'panel'))
Inputs may be any that keep to these rules, and one draw needn't show every extreme that they name: `obs_position`: observers lie at distances 6 to 12 from the anchor.
All inputs are finite; a program needn't handle non-finite values.
Results may differ from a plain program's by a relative error of at most 0.0027.
Values may be sent and summed in bfloat16 or wider, within the bound.
No kernel may reach another device: no remote copies, remote signals or barrier semaphores. Data moves between devices by JAX's collectives and lax.ppermute only.
A program may use at most 64 MiB of HBM per device.

v0:
```python
import math

import jax
import jax.numpy as jnp
from jax import lax
from jax.sharding import PartitionSpec as P

TIME = 1024
NF = 32
FBLK = 4


SPACING = 0.1


def in_blocks(shard, dim, size):
    before, after = (shard.shape[:dim], shard.shape[dim + 1 :])
    return jnp.moveaxis(shard.reshape(*before, size, -1, *after), dim, 0)


def in_order(tiles, dim):
    tiles = jnp.moveaxis(tiles, 0, dim)
    dims = tiles.shape
    return tiles.reshape(*dims[:dim], dims[dim] * dims[dim + 1], *dims[dim + 2 :])


def exchange_both(shard, axis, axes, splits, concats):
    sizes = [lax.axis_size(a) for a in axes]
    tiles = in_blocks(shard, splits[0], sizes[0])
    tiles = jnp.moveaxis(in_blocks(tiles, splits[1] + 1, sizes[1]), 0, 1)
    inside = tiles.shape[2:]
    tiles = tiles.reshape(-1, *inside)
    tiles = lax.all_to_all(tiles, axis, split_axis=0, concat_axis=0, tiled=True)
    tiles = in_order(tiles.reshape(*sizes, *inside), concats[0] + 1)
    return in_order(tiles, concats[1])


def copy_for_each(shard, axis):
    size = lax.axis_size(axis)
    return lax.all_to_all(
        jnp.broadcast_to(shard[None], (size, *shard.shape)), axis, 0, 0, tiled=True
    )


def collect(shard, axis, dim):
    return in_order(copy_for_each(shard, axis), dim)


def sum_at_owner(shard, axis, dim):
    tiles = in_blocks(shard, dim, lax.axis_size(axis))
    arrived = lax.all_to_all(tiles, axis, split_axis=0, concat_axis=0, tiled=True)
    return arrived.sum(axis=0)


def make_table(time_rows, freq_bins):
    phase_index = freq_bins[None, :] * time_rows[:, None] % TIME
    angle_arg = 2.0 * math.pi / TIME * phase_index.astype(jnp.float32)
    window = 0.5 - 0.5 * jnp.cos(2.0 * math.pi / TIME * time_rows.astype(jnp.float32))
    weight = 2.0 / TIME * window[:, None]
    return jnp.concatenate(
        [weight * jnp.cos(angle_arg), -weight * jnp.sin(angle_arg)], axis=1
    ).astype(jnp.bfloat16)


def live_rows(counts):
    lane_ids = jnp.arange(128, dtype=jnp.int32)
    return (lane_ids[None, :] < counts[:, None]).astype(jnp.float32).reshape(-1)


def transform(window_table, turned):
    flat_samples = turned.reshape(window_table.shape[0], -1)
    raw_spectra = lax.dot_general(
        window_table, flat_samples, (((0,), (0,)), ((), ())), preferred_element_type=jnp.float32
    )
    return raw_spectra.reshape(2 * NF, 4, -1)


def radiate(obs_position, panel_position, panel_area, spectra, freq_bins):
    offset = obs_position[:, :, None] - panel_position[:, None, :]
    distance = jnp.sqrt(jnp.sum(offset * offset, axis=0))
    inverse = 1.0 / distance
    unit_dir = offset * inverse[None]
    green_scale = panel_area[None, :] * inverse * (1.0 / (4.0 * math.pi))
    freq_count = freq_bins.shape[0]
    real_blocks = spectra[:freq_count].reshape(freq_count // FBLK, FBLK, 4, -1)
    imag_blocks = spectra[freq_count:].reshape(freq_count // FBLK, FBLK, 4, -1)
    bin_blocks = freq_bins.reshape(freq_count // FBLK, FBLK)

    def one_block(block_items):
        real_src, imag_src, bin_block = block_items
        wavenumber = (2.0 * math.pi / (TIME * SPACING) * bin_block.astype(jnp.float32))[
            :, None, None
        ]
        radial_real = jnp.sum(unit_dir[None] * real_src[:, 1:, None, :], axis=1)
        radial_imag = jnp.sum(unit_dir[None] * imag_src[:, 1:, None, :], axis=1)
        source_real = (
            -wavenumber * imag_src[:, 0][:, None, :]
            + radial_real * inverse[None]
            - wavenumber * radial_imag
        )
        source_imag = (
            wavenumber * real_src[:, 0][:, None, :]
            + wavenumber * radial_real
            + radial_imag * inverse[None]
        )
        phase_arg = wavenumber * distance[None]
        cosine = jnp.cos(phase_arg)
        sine_part = jnp.sin(phase_arg)
        out_real = jnp.sum(
            green_scale[None] * (cosine * source_real + sine_part * source_imag), axis=2
        )
        out_imag = jnp.sum(
            green_scale[None] * (cosine * source_imag - sine_part * source_real), axis=2
        )
        return jnp.stack([out_real, out_imag])

    result = lax.map(one_block, (real_blocks, imag_blocks, bin_blocks))
    return jnp.transpose(result, (1, 0, 2, 3)).reshape(2, freq_count, -1)


def shards(samples, panel_position, panel_area, panel_counts, obs_position, freq_bins):
    slab_len = samples.shape[0]
    panel_count = lax.axis_size("panel")
    obs_count = lax.axis_size("obs")
    source_slabs = jnp.arange(panel_count, dtype=jnp.int32)
    inner_step = jnp.arange(slab_len, dtype=jnp.int32)
    turned = exchange_both(samples, ("panel", "obs"), ("panel", "obs"), (2, 2), (0, 0))
    quarters = jnp.arange(obs_count, dtype=jnp.int32)
    time_rows = (
        (source_slabs[None, :, None] * obs_count + quarters[:, None, None]) * slab_len
        + inner_step[None, None, :]
    ).reshape(-1)
    local_spectra = transform(make_table(time_rows, freq_bins), turned)
    spectra = collect(local_spectra, "obs", 2)
    sources = spectra * live_rows(panel_counts)[None, None, :]
    partial_field = radiate(obs_position, panel_position, panel_area, sources, freq_bins)
    return sum_at_owner(partial_field, "panel", 2)


def solution(mesh):
    in_specs = (
        P(("panel", "obs"), None, None),
        P(None, "panel"),
        P("panel"),
        P("panel"),
        P(None, "obs"),
        P(),
    )
    out_specs = P(None, None, ("obs", "panel"))
    return jax.shard_map(shards, mesh=mesh, in_specs=in_specs, out_specs=out_specs, check_vma=False)
```

profile of v0, /device:TPU:1, one launch (start us, length us, event | category | flops | bytes accessed | tf_op | source)
XLA Modules:
  0.0 177.3 jit_solution(12850980860544119337)
XLA Ops:
  0.0 1.8 %reshape.144 = bf16[4,4,64,512]{3,2,1,0:T(8,128)(2,1)S(1)} reshape(bf16[4,4,32768]{2,1,0:T(4,128)(2,1)} %param.8) | data formatting | bytes 2097152 | tf_op jit(solution)/shard_map/reshape | solution.py:18
  1.8 0.3 fusion.28
  2.1 0.1 pad_maximum_fusion
  2.3 0.7 copy.44
  3.0 1.4 copy.45
  4.3 15.6 %all-to-all-start = ((bf16[256,4,4,128]{3,1,2,0:T(4,128)(2,1)}), bf16[256,4,4,128]{3,1,2,0:T(4,128)(2,1)S(1)}, u32[]{:S(2)}, u32[]{:S(2)}) async-start(bf16[256,4,4,128]{3,1,2,0:T(4,128)(2,1)} %copy.45), calls=%async_computation | async-start | bytes 2097152 | tf_op jit(solution)/shard_map/all_to_all | solution.py:33
  20.0 0.1 reshape.143
  20.1 0.1 iota_add_fusion
  20.2 0.1 add.114
  20.4 0.6 multiply_convert_fusion.1
  21.0 29.8 %all-to-all-done = bf16[256,4,4,128]{3,1,2,0:T(4,128)(2,1)S(1)} async-done(((bf16[256,4,4,128]{3,1,2,0:T(4,128)(2,1)}), bf16[256,4,4,128]{3,1,2,0:T(4,128)(2,1)S(1)}, u32[]{:S(2)}, u32[]{:S(2)}) %all-to-all-start) | async-done | bytes 1048608 | tf_op jit(solution)/shard_map/all_to_all | solution.py:33
  50.8 0.3 copy.46
  51.1 0.8 copy.47
  51.9 0.2 copy.62
  52.1 0.5 copy.48
  52.7 0.4 fusion.21
  53.1 0.1 copy.49
  53.2 0.9 broadcast_in_dim.8
  54.1 3.6 %all-to-all-start.1 = ((f32[4,64,4,128]{3,2,1,0:T(4,128)}), f32[4,64,4,128]{3,2,1,0:T(4,128)S(1)}, u32[]{:S(2)}, u32[]{:S(2)}) async-start(f32[4,64,4,128]{3,2,1,0:T(4,128)} %broadcast_in_dim.8), calls=%async_computation.1 | async-start | bytes 1048576 | tf_op jit(solution)/shard_map/all_to_all | solution.py:40
  57.8 0.2 multiply_reduce_fusion.2
  58.0 0.3 fusion.29
  58.3 8.9 %all-to-all-done.1 = f32[4,64,4,128]{3,2,1,0:T(4,128)S(1)} async-done(((f32[4,64,4,128]{3,2,1,0:T(4,128)}), f32[4,64,4,128]{3,2,1,0:T(4,128)S(1)}, u32[]{:S(2)}, u32[]{:S(2)}) %all-to-all-start.1) | async-done | bytes 524320 | tf_op jit(solution)/shard_map/all_to_all | solution.py:40
  67.2 0.3 copy.50
  67.5 0.2 reshape.147
  67.9 0.1 reshape.149
  67.9 0.1 reshape.148
  68.0 87.3 %while.11 = (s32[]{:T(128)}, f32[8,2,4,256]{3,2,1,0:T(4,128)S(1)}, f32[256,512]{1,0:T(8,128)S(1)}, s32[8,4]{1,0:T(8,128)S(1)}, f32[256,512]{1,0:T(8,128)S(1)}, /...) while((s32[]{:T(128)}, f32[8,2,4,256]{3,2,1,0:T(4,128)S(1)}, ...), condition=%wide.region_6.7_spmd.clone, body=%wide.region_1.6_spmd.clone.sunk | while | flops 15994894 | bytes 14091497 | solution.py:117
  68.2 0.1 fusion.39
  68.3 0.2 subtract_multiply_fusion.3
  68.5 1.0 multiply_reduce_fusion.4
  69.5 9.4 %fusion.40 = (f32[4,256]{1,0:T(4,128)S(1)}, f32[4,256]{1,0:T(4,128)S(1)}) fusion(f32[256,512]{1,0:T(8,128)S(1)} %get-tuple-element.257, f32[4]{0:T(128)S(1)} %get-tuple-element.221, f32[256,512]{1,0:T(8,128)S(1)} %get-tuple-element.255, f32[4,256,512]{2,1,0:T(8,128)S(1)} %get-tuple-element.224, f32[4,256,512]{2,1,0:T(8,128)S(1)} %get-tuple-element.225, ...), kind=kLoop, calls=%fused_computation.11.clone.1 | loop fusion | flops 9959424 | bytes 5791760 | tf_op jit(solution)/shard_map/while/body/eval_jaxpr/reduce_sum | solution.py:109
  79.1 0.1 fusion.39
  79.2 0.2 subtract_multiply_fusion.3
  79.4 1.0 multiply_reduce_fusion.4
  80.4 9.4 %fusion.40 = (f32[4,256]{1,0:T(4,128)S(1)}, f32[4,256]{1,0:T(4,128)S(1)}) fusion(f32[256,512]{1,0:T(8,128)S(1)} %get-tuple-element.257, f32[4]{0:T(128)S(1)} %get-tuple-element.221, f32[256,512]{1,0:T(8,128)S(1)} %get-tuple-element.255, f32[4,256,512]{2,1,0:T(8,128)S(1)} %get-tuple-element.224, f32[4,256,512]{2,1,0:T(8,128)S(1)} %get-tuple-element.225, ...), kind=kLoop, calls=%fused_computation.11.clone.1 | loop fusion | flops 9959424 | bytes 5791760 | tf_op jit(solution)/shard_map/while/body/eval_jaxpr/reduce_sum | solution.py:109
  90.0 0.1 fusion.39
  90.1 0.2 subtract_multiply_fusion.3
  90.3 1.0 multiply_reduce_fusion.4
  91.3 9.4 %fusion.40 = (f32[4,256]{1,0:T(4,128)S(1)}, f32[4,256]{1,0:T(4,128)S(1)}) fusion(f32[256,512]{1,0:T(8,128)S(1)} %get-tuple-element.257, f32[4]{0:T(128)S(1)} %get-tuple-element.221, f32[256,512]{1,0:T(8,128)S(1)} %get-tuple-element.255, f32[4,256,512]{2,1,0:T(8,128)S(1)} %get-tuple-element.224, f32[4,256,512]{2,1,0:T(8,128)S(1)} %get-tuple-element.225, ...), kind=kLoop, calls=%fused_computation.11.clone.1 | loop fusion | flops 9959424 | bytes 5791760 | tf_op jit(solution)/shard_map/while/body/eval_jaxpr/reduce_sum | solution.py:109
  101.0 0.2 subtract_multiply_fusion.3
  101.2 1.0 multiply_reduce_fusion.4
  102.2 9.4 %fusion.40 = (f32[4,256]{1,0:T(4,128)S(1)}, f32[4,256]{1,0:T(4,128)S(1)}) fusion(f32[256,512]{1,0:T(8,128)S(1)} %get-tuple-element.257, f32[4]{0:T(128)S(1)} %get-tuple-element.221, f32[256,512]{1,0:T(8,128)S(1)} %get-tuple-element.255, f32[4,256,512]{2,1,0:T(8,128)S(1)} %get-tuple-element.224, f32[4,256,512]{2,1,0:T(8,128)S(1)} %get-tuple-element.225, ...), kind=kLoop, calls=%fused_computation.11.clone.1 | loop fusion | flops 9959424 | bytes 5791760 | tf_op jit(solution)/shard_map/while/body/eval_jaxpr/reduce_sum | solution.py:109
  111.8 0.1 fusion.39
  111.9 0.2 subtract_multiply_fusion.3
  112.1 1.0 multiply_reduce_fusion.4
  113.1 9.4 %fusion.40 = (f32[4,256]{1,0:T(4,128)S(1)}, f32[4,256]{1,0:T(4,128)S(1)}) fusion(f32[256,512]{1,0:T(8,128)S(1)} %get-tuple-element.257, f32[4]{0:T(128)S(1)} %get-tuple-element.221, f32[256,512]{1,0:T(8,128)S(1)} %get-tuple-element.255, f32[4,256,512]{2,1,0:T(8,128)S(1)} %get-tuple-element.224, f32[4,256,512]{2,1,0:T(8,128)S(1)} %get-tuple-element.225, ...), kind=kLoop, calls=%fused_computation.11.clone.1 | loop fusion | flops 9959424 | bytes 5791760 | tf_op jit(solution)/shard_map/while/body/eval_jaxpr/reduce_sum | solution.py:109
  122.8 0.2 subtract_multiply_fusion.3
  123.0 1.0 multiply_reduce_fusion.4
  124.0 9.4 %fusion.40 = (f32[4,256]{1,0:T(4,128)S(1)}, f32[4,256]{1,0:T(4,128)S(1)}) fusion(f32[256,512]{1,0:T(8,128)S(1)} %get-tuple-element.257, f32[4]{0:T(128)S(1)} %get-tuple-element.221, f32[256,512]{1,0:T(8,128)S(1)} %get-tuple-element.255, f32[4,256,512]{2,1,0:T(8,128)S(1)} %get-tuple-element.224, f32[4,256,512]{2,1,0:T(8,128)S(1)} %get-tuple-element.225, ...), kind=kLoop, calls=%fused_computation.11.clone.1 | loop fusion | flops 9959424 | bytes 5791760 | tf_op jit(solution)/shard_map/while/body/eval_jaxpr/reduce_sum | solution.py:109
  133.7 0.2 subtract_multiply_fusion.3
  133.9 1.0 multiply_reduce_fusion.4
  134.9 9.4 %fusion.40 = (f32[4,256]{1,0:T(4,128)S(1)}, f32[4,256]{1,0:T(4,128)S(1)}) fusion(f32[256,512]{1,0:T(8,128)S(1)} %get-tuple-element.257, f32[4]{0:T(128)S(1)} %get-tuple-element.221, f32[256,512]{1,0:T(8,128)S(1)} %get-tuple-element.255, f32[4,256,512]{2,1,0:T(8,128)S(1)} %get-tuple-element.224, f32[4,256,512]{2,1,0:T(8,128)S(1)} %get-tuple-element.225, ...), kind=kLoop, calls=%fused_computation.11.clone.1 | loop fusion | flops 9959424 | bytes 5791760 | tf_op jit(solution)/shard_map/while/body/eval_jaxpr/reduce_sum | solution.py:109
  144.5 0.1 fusion.39
  144.6 0.2 subtract_multiply_fusion.3
  144.8 1.0 multiply_reduce_fusion.4
  145.9 9.4 %fusion.40 = (f32[4,256]{1,0:T(4,128)S(1)}, f32[4,256]{1,0:T(4,128)S(1)}) fusion(f32[256,512]{1,0:T(8,128)S(1)} %get-tuple-element.257, f32[4]{0:T(128)S(1)} %get-tuple-element.221, f32[256,512]{1,0:T(8,128)S(1)} %get-tuple-element.255, f32[4,256,512]{2,1,0:T(8,128)S(1)} %get-tuple-element.224, f32[4,256,512]{2,1,0:T(8,128)S(1)} %get-tuple-element.225, ...), kind=kLoop, calls=%fused_computation.11.clone.1 | loop fusion | flops 9959424 | bytes 5791760 | tf_op jit(solution)/shard_map/while/body/eval_jaxpr/reduce_sum | solution.py:109
  155.3 2.2 %reshape_reshape.3 = f32[2,32,64,4]{3,2,1,0:T(8,128)S(1)} reshape(f32[2,8,4,256]{3,2,1,0:T(4,128)S(1)} %copy.53) | data formatting | bytes 131072 | tf_op jit(solution)/shard_map/reshape;reshape | solution.py:18
  157.5 1.4 copy.54
  158.9 0.2 reshape.152
  159.1 16.0 %all_to_all.15 = f32[64,1,256]{2,1,0:T(1,128)S(1)} all-to-all(f32[64,1,256]{2,1,0:T(1,128)S(1)} %reshape.152), channel_id=1, replica_groups=mesh['panel'=64,'obs'=4] {'panel'}, dimensions={0} | all-to-all | bytes 131072 | tf_op jit(solution)/shard_map/all_to_all | solution.py:51
  175.1 0.5 broadcast.111
  175.6 0.8 reduce
  176.4 0.2 reshape.153
  176.6 0.7 bitcast_reduce_fusion
  (85 shorter events, 1.7 us)
Async XLA Ops:
  2.9 17.0 %copy-start.2 = (s32[32]{0:T(128)S(1)}, s32[32]{0:T(128)}, u32[]{:S(2)}) copy-start(s32[32]{0:T(128)} %param.13) | copy-start | bytes 388
  3.0 17.4 %copy-start.4 = (s32[4]{0:T(128)S(1)}, s32[4]{0:T(128)}, u32[]{:S(2)}) copy-start(s32[4]{0:T(128)} %param.11) | copy-start | bytes 52
  4.3 46.5 %all-to-all-start = ((bf16[256,4,4,128]{3,1,2,0:T(4,128)(2,1)}), bf16[256,4,4,128]{3,1,2,0:T(4,128)(2,1)S(1)}, u32[]{:S(2)}, u32[]{:S(2)}) async-start(bf16[256,4,4,128]{3,1,2,0:T(4,128)(2,1)} %copy.45), calls=%async_computation | async-start | bytes 2097152 | tf_op jit(solution)/shard_map/all_to_all | solution.py:33
  52.7 5.1 %copy-start = (f32[3,512]{1,0:T(4,128)S(1)}, f32[3,512]{1,0:T(4,128)}, u32[]{:S(2)}) copy-start(f32[3,512]{1,0:T(4,128)} %param.9) | copy-start | bytes 18436
  52.7 5.1 %copy-start.1 = (f32[3,256]{1,0:T(4,128)S(1)}, f32[3,256]{1,0:T(4,128)}, u32[]{:S(2)}) copy-start(f32[3,256]{1,0:T(4,128)} %param.12) | copy-start | bytes 9220
  52.7 5.3 %copy-start.3 = (f32[512]{0:T(512)S(1)}, f32[512]{0:T(512)}, u32[]{:S(2)}) copy-start(f32[512]{0:T(512)} %param.10) | copy-start | bytes 6148
  54.1 13.1 %all-to-all-start.1 = ((f32[4,64,4,128]{3,2,1,0:T(4,128)}), f32[4,64,4,128]{3,2,1,0:T(4,128)S(1)}, u32[]{:S(2)}, u32[]{:S(2)}) async-start(f32[4,64,4,128]{3,2,1,0:T(4,128)} %broadcast_in_dim.8), calls=%async_computation.1 | async-start | bytes 1048576 | tf_op jit(solution)/shard_map/all_to_all | solution.py:40
where the time goes:
time: 178 us; the launch traced here: 177 us
  other arithmetic  89.4 us (50%)
  waiting for transfers between devices  38.7 us (22%)
  starting transfers between devices  19.3 us (11%)
  blocking collectives  16 us (9%)
  local copies, waits for them, and re-layouts  12.7 us (7%)
    reduce_sum x8, other arithmetic, one_block(): jnp.sum(green_scale[None] * (cosine * source_real + sine_part * source_im...  75.3 us
    all_to_all x1, waiting for transfers between devices, exchange_both(): tiles = lax.all_to_all(tiles, axis, split_axis=0, concat_axis=0, tiled=True)  29.8 us
    all_to_all x1, blocking collectives, sum_at_owner(): lax.all_to_all(tiles, axis, split_axis=0, concat_axis=0, tiled=True)  16 us
    all_to_all x1, starting transfers between devices, exchange_both(): tiles = lax.all_to_all(tiles, axis, split_axis=0, concat_axis=0, tiled=True)  15.6 us
    all_to_all x1, waiting for transfers between devices, copy_for_each(): lax.all_to_all(jnp.broadcast_to(shard[None], (size, *shard.shape)), axis,...  8.9 us
    reduce_sum x8, other arithmetic, one_block(): radial_real = jnp.sum(unit_dir[None] * real_src[:, 1:, None, :], axis=1)  8.15 us
    all_to_all x1, starting transfers between devices, copy_for_each(): lax.all_to_all(jnp.broadcast_to(shard[None], (size, *shard.shape)), axis,...  3.65 us
  transfers between devices with their start and end apart: 2, of which 2 were waited for; matrix products, arithmetic and copies ran while one was open for 1% of the time, Pallas kernels for 0%

commit v1 on v0

v1 whole, which is shorter than its diff:
```python
import math

import jax
import jax.numpy as jnp
from jax import lax
from jax.experimental import pallas as pl
from jax.experimental.pallas import tpu as pltpu
from jax.sharding import PartitionSpec as P

TIME = 1024
NF = 32
SPACING = 0.1
LANES = 128
CHANNELS = 4
BLOCKS = 8
TILE = 32
DEPTH = 8
SLOT = 16

SIN_COEFFS = (
    4.442882919199695,
    -7.308245696158815,
    3.60635441147954,
    -0.8461128860931261,
    0.10982698817978952,
)
COS_COEFFS = (
    1.4142134965649862,
    -6.978850988235484,
    5.7394611706121585,
    -1.8835629868567052,
    0.31069819092073886,
)

VMEM = pl.BlockSpec(memory_space=pltpu.VMEM)
SMEM = pl.BlockSpec(memory_space=pltpu.SMEM)


def horner(square, coeffs):
    total = square * coeffs[-1] + coeffs[-2]
    for coeff in coeffs[-3::-1]:
        total = total * square + coeff
    return total


def turn(cycles):
    part = cycles - jnp.round(cycles)
    square = part * part
    return part * horner(square, SIN_COEFFS), horner(square, COS_COEFFS)


def arrange_kernel(x_ref, o_ref):
    for panel_block in range(x_ref.shape[2] // LANES):
        for step in range(x_ref.shape[0]):
            o_ref[panel_block, step] = x_ref[step, :, panel_block * LANES : (panel_block + 1) * LANES]


def arrange(samples):
    steps, channels, panels = samples.shape
    chunk = 4096
    return pl.pallas_call(
        arrange_kernel,
        grid=(panels // chunk,),
        in_specs=[pl.BlockSpec((steps, channels, chunk), lambda i: (0, 0, i))],
        out_specs=pl.BlockSpec((chunk // LANES, steps, channels, LANES), lambda i: (i, 0, 0, 0)),
        out_shape=jax.ShapeDtypeStruct((panels // LANES, steps, channels, LANES), samples.dtype),
        name="arrange",
    )(samples)


def bins_of_block(bins_smem, b):
    row = lax.broadcasted_iota(jnp.int32, (8, LANES), 0) % 4
    bins = [jnp.full((8, LANES), bins_smem[4 * b + i], jnp.int32) for i in range(4)]
    chosen = jnp.where(row == 0, bins[0], jnp.where(row == 1, bins[1], jnp.where(row == 2, bins[2], bins[3])))
    return chosen.astype(jnp.float32)


def wave_copy(held_ref, waves_ref, sem, slot, rows, lanes):
    return pltpu.make_async_copy(held_ref.at[slot], waves_ref.at[:, :, rows, lanes], sem.at[slot])


def prepare_kernel(
    bins_smem,
    place_smem,
    obs_ref,
    panel_ref,
    waves_ref,
    inverse_ref,
    spread_ref,
    table_ref,
    pick_ref,
    column_ref,
    fine_ref,
    coarse_ref,
    held_ref,
    sem,
):
    start = pl.multiple_of(place_smem[0] * LANES, LANES)
    mine = panel_ref[:, pl.ds(start, LANES)]
    column_ref[...] = jnp.concatenate([mine, jnp.zeros((5, LANES), jnp.float32)], axis=0).T

    groups = obs_ref.shape[1] // LANES

    def one_tile(step, carry):
        row_tile, lane_tile, slot = step // groups, step % groups, step % 2
        rows = pl.ds(pl.multiple_of(row_tile * TILE, TILE), TILE)
        lanes = pl.ds(pl.multiple_of(lane_tile * LANES, LANES), LANES)
        offsets = [obs_ref[c : c + 1, lanes] - column_ref[rows, c : c + 1] for c in range(3)]
        square = offsets[0] * offsets[0] + offsets[1] * offsets[1] + offsets[2] * offsets[2]
        inverse = lax.rsqrt(square)
        inverse_ref[rows, lanes] = inverse
        cycles = square * inverse * (1.0 / (TIME * SPACING))

        sine, cosine = turn(cycles)
        sines, cosines = sine * cosine, 1.0 - sine * sine
        double = cosines + cosines
        fine = [(inverse, jnp.zeros_like(inverse)), (inverse * cosines, inverse * sines)]
        for n in range(2, 17):
            fine.append(tuple(double * fine[n - 1][i] - fine[n - 2][i] for i in range(2)))
        for n in range(17):
            fine_ref[16 + n, 0] = fine[n][0]
            fine_ref[16 + n, 1] = fine[n][1]
            if n:
                fine_ref[16 - n, 0] = fine[n][0]
                fine_ref[16 - n, 1] = -fine[n][1]

        sine, cosine = turn(cycles * 32.0)
        coarse = [(jnp.ones_like(inverse), jnp.zeros_like(inverse)), (1.0 - sine * sine, sine * cosine)]
        for n in range(1, 9):
            twice = coarse[n][0] + coarse[n][0]
            coarse.append((twice * coarse[n][0] - 1.0, twice * coarse[n][1]))
            if n < 8:
                coarse.append(
                    (twice * coarse[n + 1][0] - coarse[1][0], twice * coarse[n + 1][1] - coarse[1][1])
                )
        for n in range(17):
            coarse_ref[n, 0] = coarse[n][0]
            coarse_ref[n, 1] = coarse[n][1]

        @pl.when(step >= 2)
        def _():
            wave_copy(held_ref, waves_ref, sem, slot, 0, 0).wait()

        for j in range(NF):
            bin_number = bins_smem[j]
            whole = (bin_number + 16) >> 5
            rest = bin_number - (whole << 5) + 16
            c0, s0 = coarse_ref[whole, 0], coarse_ref[whole, 1]
            c1, s1 = fine_ref[rest, 0], fine_ref[rest, 1]
            held_ref[slot, j, 0] = c0 * c1 - s0 * s1
            held_ref[slot, j, 1] = s0 * c1 + c0 * s1
        wave_copy(held_ref, waves_ref, sem, slot, row_tile, lane_tile).start()
        return carry

    steps = (LANES // TILE) * groups
    lax.fori_loop(0, steps, one_tile, 0)

    obs = obs_ref[...]
    high = obs.astype(jnp.bfloat16).astype(jnp.float32)
    low = obs - high
    minus = jnp.full((6, obs.shape[1]), -1.0, jnp.float32)
    slot_rows = jnp.concatenate([high, high, low, minus, jnp.zeros((1, obs.shape[1]), jnp.float32)], axis=0)
    spread_ref[...] = jnp.zeros_like(spread_ref)
    for s in range(8):
        spread_ref[s, s * SLOT : (s + 1) * SLOT, :] = slot_rows.astype(jnp.bfloat16)

    rows = 2 * NF

    def one_chunk(chunk, carry):
        start = pl.multiple_of(chunk * LANES, LANES)
        column = lax.broadcasted_iota(jnp.int32, (8, LANES), 1) + start
        time = (column >> 2).astype(jnp.float32)
        channel = column & 3
        sine, cosine = turn(time * (1.0 / TIME))
        weight = (2.0 / TIME) * (0.5 * (sine * sine))
        is_real = lax.broadcasted_iota(jnp.int32, (8, LANES), 0) < 4
        values = []
        for b in range(BLOCKS):
            sine, cosine = turn(bins_of_block(bins_smem, b) * time * (1.0 / TIME))
            values.append(weight * jnp.where(is_real, 1.0 - sine * sine, -(sine * cosine)))
        values = jnp.concatenate(values, axis=0)
        channels = jnp.concatenate([channel] * BLOCKS, axis=0)
        for c in range(CHANNELS):
            table_ref[c * rows : (c + 1) * rows, pl.ds(start, LANES)] = jnp.where(
                channels == (c + 1) % CHANNELS, values, 0.0
            ).astype(jnp.bfloat16)
        return carry

    lax.fori_loop(0, TIME * CHANNELS // LANES, one_chunk, 0)

    source = lax.broadcasted_iota(jnp.int32, (rows, pick_ref.shape[1]), 0)
    target = lax.broadcasted_iota(jnp.int32, (rows, pick_ref.shape[1]), 1)
    same = jnp.where((target >> 4) == source, 1.0, 0.0)
    slot = lax.broadcasted_iota(jnp.int32, (8, pick_ref.shape[1]), 1) & 15
    for piece, bases in enumerate(((0, 6), (3, 3), (9, 9), (12, 12))):
        for direction in range(4):
            first = piece * 256 + direction * rows
            if direction == 3:
                pick_ref[first : first + rows, :] = jnp.zeros((rows, pick_ref.shape[1]), jnp.bfloat16)
                continue
            match = (slot == bases[0] + direction) | (slot == bases[1] + direction)
            chosen = jnp.where(match, 1.0, 0.0)
            pick_ref[first : first + rows, :] = (same * chosen[0:1]).astype(jnp.bfloat16)

    for step in (steps - 2, steps - 1):
        wave_copy(held_ref, waves_ref, sem, step % 2, 0, 0).wait()


def prepare(bins, place, obs, panel_position):
    observers = obs.shape[1]
    f32 = jnp.float32
    return pl.pallas_call(
        prepare_kernel,
        in_specs=[SMEM, SMEM, VMEM, VMEM],
        out_specs=[pl.BlockSpec(memory_space=pl.ANY)] + [VMEM] * 5,
        out_shape=[
            jax.ShapeDtypeStruct((NF, 2, LANES // TILE, observers // LANES, TILE, LANES), f32),
            jax.ShapeDtypeStruct((LANES, observers), f32),
            jax.ShapeDtypeStruct((8, LANES, observers), jnp.bfloat16),
            jax.ShapeDtypeStruct((CHANNELS * 2 * NF, CHANNELS * TIME), jnp.bfloat16),
            jax.ShapeDtypeStruct((1024, 1024), jnp.bfloat16),
            jax.ShapeDtypeStruct((LANES, 8), f32),
        ],
        scratch_shapes=[
            pltpu.VMEM((33, 2, TILE, LANES), f32),
            pltpu.VMEM((17, 2, TILE, LANES), f32),
            pltpu.VMEM((2, NF, 2, TILE, LANES), f32),
            pltpu.SemaphoreType.DMA((2,)),
        ],
        cost_estimate=pl.CostEstimate(flops=20_000_000_000, bytes_accessed=40_000_000, transcendentals=0),
        compiler_params=pltpu.CompilerParams(vmem_limit_bytes=32 << 20),
        name="prepare",
    )(bins, place, obs, panel_position)


def wave_fetch(waves_ref, held_ref, sem, j, slot):
    return pltpu.make_async_copy(waves_ref.at[j], held_ref.at[slot], sem.at[slot])


def radiate_kernel(
    bins_smem,
    data_ref,
    waves_ref,
    inverse_ref,
    spread_ref,
    table_ref,
    pick_ref,
    column_ref,
    scale_ref,
    o_ref,
    left_ref,
    mono_ref,
    product_ref,
    field_ref,
    held_ref,
    sem,
):
    for j in range(DEPTH):
        wave_fetch(waves_ref, held_ref, sem, j, j).start()
    spectra = jnp.dot(table_ref[...], data_ref[...], preferred_element_type=jnp.float32)
    scales = [
        bins_of_block(bins_smem, b) * (2.0 * math.pi / (TIME * SPACING)) * scale_ref[...] for b in range(BLOCKS)
    ]
    turned = (spectra * jnp.concatenate(scales * CHANNELS, axis=0)).T
    lane = lax.broadcasted_iota(jnp.int32, turned.shape, 1)
    position = jnp.where(
        lane < 64, column_ref[:, 0:1], jnp.where(lane < 128, column_ref[:, 1:2], column_ref[:, 2:3])
    )
    moment = turned * position
    high = turned.astype(jnp.bfloat16)
    low = (turned - high.astype(jnp.float32)).astype(jnp.bfloat16)
    moment_high = moment.astype(jnp.bfloat16)
    moment_low = (moment - moment_high.astype(jnp.float32)).astype(jnp.bfloat16)
    pieces = jnp.concatenate([high, low, moment_high, moment_low], axis=1)
    slots = jnp.dot(pieces, pick_ref[...], preferred_element_type=jnp.float32).astype(jnp.bfloat16)
    for b in range(BLOCKS):
        left_ref[b] = slots[:, b * LANES : (b + 1) * LANES]
        mono_ref[b, :, 0:8] = turned[:, 192 + 8 * b : 200 + 8 * b]

    panels = inverse_ref.shape[0]
    width = 256

    def one_block(b, carry):
        left = left_ref[b]
        for jj in range(4):
            j = b * 4 + jj
            held = (b % 2) * 4 + jj
            wave = jnp.full((8, LANES), bins_smem[j], jnp.int32).astype(jnp.float32)
            inverse_wave = 1.0 / (wave * (2.0 * math.pi / (TIME * SPACING)))
            mono_real = jnp.broadcast_to(mono_ref[b, :, jj : jj + 1], (panels, LANES))
            mono_imag = jnp.broadcast_to(mono_ref[b, :, 4 + jj : 5 + jj], (panels, LANES))
            wave_fetch(waves_ref, held_ref, sem, j, held).wait()
            for t in range(inverse_ref.shape[1] // width):
                parity = t % 2
                columns = slice(t * width, (t + 1) * width)
                product_ref[parity, 0] = jnp.dot(
                    left, spread_ref[jj, :, columns], preferred_element_type=jnp.float32
                )
                product_ref[parity, 1] = jnp.dot(
                    left, spread_ref[4 + jj, :, columns], preferred_element_type=jnp.float32
                )
                for half in range(2):
                    inner = slice(half * LANES, (half + 1) * LANES)
                    lane_tile = t * 2 + half
                    lanes = slice(lane_tile * LANES, (lane_tile + 1) * LANES)
                    sum_real = jnp.zeros((8, LANES), jnp.float32)
                    sum_imag = jnp.zeros((8, LANES), jnp.float32)
                    for p in range(panels // 8):
                        rows = slice(p * 8, p * 8 + 8)
                        row_tile, inside = p * 8 // TILE, slice(p * 8 % TILE, p * 8 % TILE + 8)
                        inverse = inverse_ref[rows, lanes]
                        cosine = held_ref[held, 0, row_tile, lane_tile, inside]
                        sine = held_ref[held, 1, row_tile, lane_tile, inside]
                        radial_real = product_ref[parity, 0, rows, inner] * inverse
                        radial_imag = product_ref[parity, 1, rows, inner] * inverse
                        near = inverse * inverse_wave
                        source_real = near * radial_real - (mono_imag[rows] + radial_imag)
                        source_imag = near * radial_imag + (mono_real[rows] + radial_real)
                        sum_real = sum_real + (cosine * source_real + sine * source_imag)
                        sum_imag = sum_imag + (cosine * source_imag - sine * source_real)
                    row = jj * 4 + t
                    field_ref[b, 0, row : row + 1, inner] = jnp.sum(sum_real, axis=0, keepdims=True)
                    field_ref[b, 1, row : row + 1, inner] = jnp.sum(sum_imag, axis=0, keepdims=True)

            @pl.when(j + DEPTH < NF)
            def _():
                wave_fetch(waves_ref, held_ref, sem, j + DEPTH, held).start()

        return carry

    lax.fori_loop(0, BLOCKS, one_block, 0)
    for part in range(2):
        flat = jnp.concatenate([field_ref[b, part] for b in range(BLOCKS)], axis=0)
        o_ref[:, part, :] = flat.T


def radiate(bins, data, prepared, scale):
    panels, observers = prepared[1].shape
    return pl.pallas_call(
        radiate_kernel,
        in_specs=[SMEM, VMEM, pl.BlockSpec(memory_space=pl.ANY)] + [VMEM] * 6,
        out_specs=VMEM,
        out_shape=jax.ShapeDtypeStruct((observers // 4, 2, LANES), jnp.float32),
        scratch_shapes=[
            pltpu.VMEM((BLOCKS, panels, LANES), jnp.bfloat16),
            pltpu.VMEM((BLOCKS, panels, LANES), jnp.float32),
            pltpu.VMEM((2, 2, panels, 256), jnp.float32),
            pltpu.VMEM((BLOCKS, 2, 16, 256), jnp.float32),
            pltpu.VMEM((DEPTH, 2, panels // TILE, observers // LANES, TILE, LANES), jnp.float32),
            pltpu.SemaphoreType.DMA((DEPTH,)),
        ],
        cost_estimate=pl.CostEstimate(flops=20_000_000_000, bytes_accessed=40_000_000, transcendentals=0),
        compiler_params=pltpu.CompilerParams(vmem_limit_bytes=40 << 20),
        name="radiate",
    )(bins, data, *prepared, scale)


def gather_kernel(x_ref, o_ref):
    total = jnp.sum(x_ref[...], axis=0)
    lane = lax.broadcasted_iota(jnp.int32, (NF, LANES), 1)
    row = lax.broadcasted_iota(jnp.int32, (NF, LANES), 0)
    for part in range(2):
        for i in range(4):
            o_ref[part, :, i : i + 1] = jnp.sum(
                jnp.where(lane == row * 4 + i, total[part : part + 1, :], 0.0), axis=1, keepdims=True
            )


def gather(arrived):
    return pl.pallas_call(
        gather_kernel,
        in_specs=[VMEM],
        out_specs=VMEM,
        out_shape=jax.ShapeDtypeStruct((2, NF, 4), jnp.float32),
        name="gather",
    )(arrived)


def all_observers(obs_position):
    whole = lax.all_gather(obs_position, "obs")
    whole = whole.reshape(lax.axis_size("obs"), 3, lax.axis_size("panel"), 4)
    return jnp.transpose(whole, (1, 3, 2, 0)).reshape(3, -1)


def local_field(data, place, panel_position, scale, observers, bins):
    prepared = prepare(bins, place, observers, panel_position)
    return radiate(bins, data, prepared, scale)


def shards(samples, panel_position, panel_area, panel_counts, obs_position, freq_bins):
    arrived = lax.all_to_all(arrange(samples), ("panel", "obs"), 0, 0, tiled=True)
    data = arrived.reshape(-1, LANES)

    place = lax.axis_index("obs")
    area = lax.dynamic_slice_in_dim(panel_area, place * LANES, LANES, 0)
    count = lax.dynamic_slice_in_dim(panel_counts, place, 1, 0)
    lane_ids = jnp.arange(LANES, dtype=jnp.int32)
    scale = jnp.where(lane_ids < count, area * (1.0 / (4.0 * math.pi)), 0.0)[None, :]

    observers = all_observers(obs_position)
    partial = local_field(data, place.reshape(1), panel_position, scale, observers, freq_bins)
    return gather(lax.all_to_all(partial, ("panel", "obs"), 0, 0, tiled=True))


def solution(mesh):
    in_specs = (
        P(("panel", "obs"), None, None),
        P(None, "panel"),
        P("panel"),
        P("panel"),
        P(None, "obs"),
        P(),
    )
    out_specs = P(None, None, ("obs", "panel"))
    return jax.shard_map(shards, mesh=mesh, in_specs=in_specs, out_specs=out_specs, check_vma=False)
```

time: 178 us -> 116 us (0.65)
  other arithmetic: 89.4 us -> 1.39 us
  Pallas kernels: 0 us -> 46.1 us
  waiting for transfers between devices: 38.7 us -> 0.01 us
  blocking collectives: 16 us -> 40.8 us
  starting transfers between devices: 19.3 us -> 15.6 us
    reduce_sum x18 -> x0, other arithmetic: 84.3 us -> none  [the longest x8 75.3 us: one_block(): jnp.sum(green_scale[None] * (cosine * source_real + sine_part * source_im...]
    pallas_call x0 -> x4, Pallas kernels: none -> 46.1 us  [the longest x1 19.7 us: prepare(): pl.pallas_call(prepare_kernel, in_specs=[SMEM, SMEM, VMEM, VMEM], out_spe...]
    all_to_all x2 -> x1, waiting for transfers between devices: 38.7 us -> 0.01 us  [shards(): lax.all_to_all(arrange(samples), ('panel', 'obs'), 0, 0, tiled=True)]
    all_to_all x1, blocking collectives: 16 us -> 30.4 us  [shards(): return gather(lax.all_to_all(partial, ('panel', 'obs'), 0, 0, tiled=True))]
    all_gather x0 -> x1, blocking collectives: none -> 10.4 us  [all_observers(): whole = lax.all_gather(obs_position, 'obs')]
    unnamed x13 -> x20, local copies, waits for them, and re-layouts: 0.58 us -> 7.74 us
    all_to_all x2 -> x1, starting transfers between devices: 19.3 us -> 15.6 us  [shards(): lax.all_to_all(arrange(samples), ('panel', 'obs'), 0, 0, tiled=True)]
    reshape x6 -> x2, local copies, waits for them, and re-layouts: 3.6 us -> 0.66 us  [the longest x1 0.4 us: all_observers(): whole = whole.reshape(lax.axis_size('obs'), 3, lax.axis_size('panel'), 4)]
  transfers between devices with their start and end apart: 2 -> 1, of which waited for: 2 -> 0; matrix products, arithmetic and copies ran while one was open for 1% -> 4% of each run, Pallas kernels for 0% -> 17%
where the time goes in v1:
time: 116 us
  Pallas kernels  46.1 us (40%)
  blocking collectives  40.8 us (35%)
  starting transfers between devices  15.6 us (13%)
  local copies, waits for them, and re-layouts  11.9 us (10%)
  other arithmetic  1.39 us (1%)
    all_to_all x1, blocking collectives, shards(): return gather(lax.all_to_all(partial, ('panel', 'obs'), 0, 0, tiled=True))  30.4 us
    pallas_call x1, Pallas kernels, prepare(): pl.pallas_call(prepare_kernel, in_specs=[SMEM, SMEM, VMEM, VMEM], out_spe...  19.7 us
    pallas_call x1, Pallas kernels, radiate(): pl.pallas_call(radiate_kernel, in_specs=[SMEM, VMEM, pl.BlockSpec(memory_...  19.2 us
    all_to_all x1, starting transfers between devices, shards(): lax.all_to_all(arrange(samples), ('panel', 'obs'), 0, 0, tiled=True)  15.6 us
    all_gather x1, blocking collectives, all_observers(): whole = lax.all_gather(obs_position, 'obs')  10.4 us
    unnamed x20, local copies, waits for them, and re-layouts  7.74 us
    pallas_call x1, Pallas kernels, arrange(): pl.pallas_call(arrange_kernel, grid=(panels // chunk,), in_specs=[pl.Bloc...  5.32 us
  transfers between devices with their start and end apart: 1, of which 0 were waited for; matrix products, arithmetic and copies ran while one was open for 4% of the time, Pallas kernels for 17%

profile of v1, /device:TPU:1, one launch (start us, length us, event | category | flops | bytes accessed | tf_op | source)
XLA Modules:
  0.0 115.9 jit_solution(15616365072149416453)
XLA Ops:
  0.0 0.0 copy-start.8
  0.0 5.3 %arrange.1 = bf16[256,4,4,128]{3,2,1,0:T(4,128)(2,1)} custom-call(bf16[4,4,32768]{2,1,0:T(4,128)(2,1)} %x_ref.1), custom_call_target="tpu_custom_call" | custom-call | tf_op jit(solution)/shard_map/arrange/pallas_call | solution.py:61
  5.3 0.0 copy-start.9
  5.3 0.0 copy-start
  5.3 0.0 copy-start.1
  5.3 15.6 %all-to-all-start = ((bf16[256,4,4,128]{3,2,1,0:T(4,128)(2,1)}), bf16[256,4,4,128]{3,2,1,0:T(4,128)(2,1)S(1)}, u32[]{:S(2)}, u32[]{:S(2)}) async-start(bf16[256,4,4,128]{3,2,1,0:T(4,128)(2,1)} %arrange.1), calls=%async_computation | async-start | bytes 2097152 | tf_op jit(solution)/shard_map/all_to_all | solution.py:391
  21.0 0.0 copy-done.8
  21.0 10.4 %all-gather.1 = f32[4,3,256]{2,1,0:T(4,128)S(1)} all-gather(f32[1,3,256]{2,1,0:T(4,128)S(1)} %bitcast.13), channel_id=2, replica_groups=mesh['panel'=64,'obs'=4] {'obs'}, dimensions={0}, use_global_device_ids=true | all-gather | bytes 15360 | tf_op jit(solution)/shard_map/all_gather | solution.py:380
  31.4 0.4 reshape.14
  31.8 1.5 %copy.13 = f32[3,4,64,4]{3,2,1,0:T(8,128)S(1)} copy(f32[3,4,64,4]{1,2,3,0:T(8,128)S(1)} %bitcast.12) | data formatting | bytes 24576 | tf_op jit(solution)/shard_map/transpose | solution.py:382
  33.3 0.3 reshape.15.obs_ref
  33.5 0.0 copy-done.9
  33.6 0.6 dynamic_slice.6
  34.2 1.4 %fusion.scale_ref = f32[1,128]{1,0:T(1,128)S(1)} fusion(f32[512]{0:T(512)} %param.8, s32[]{:T(128)S(6)} %select_n.11, s32[]{:T(128)} %bitcast.4), kind=kLoop, calls=%fused_computation.1 | loop fusion | flops 384 | bytes 1032 | tf_op jit(solution)/shard_map/broadcast_in_dim | solution.py:398
  35.6 0.0 copy-done
  35.6 0.0 copy-done.1
  35.6 19.7 %prepare.1 = (f32[32,2,4,8,32,128]{5,4,3,2,1,0:T(8,128)}, f32[128,1024]{1,0:T(8,128)S(1)}, bf16[8,128,1024]{2,1,0:T(8,128)(2,1)S(1)}, bf16[256,4096]{1,0:T(8,128...) custom-call(s32[32]{0:T(128)S(1)} %copy-done.1, s32[1]{0:T(128)} %bitcast.1.place_smem, ...), custom_call_target="tpu_custom_call" | custom-call | flops 20000000000 | bytes 40000000 | tf_op jit(solution)/shard_map/prepare/pallas_call | solution.py:212
  55.2 0.0 copy-start.2
  55.2 1.3 %copy-done.2 = bf16[256,4096]{1,0:T(8,128)(2,1)} copy-done((bf16[256,4096]{1,0:T(8,128)(2,1)}, bf16[256,4096]{1,0:T(8,128)(2,1)S(1)}, u32[]{:S(2)}) %copy-start.2) | copy-done | bytes 2097176
  56.6 0.0 copy-start.4
  56.6 1.4 %copy-done.4 = bf16[1024,1024]{1,0:T(8,128)(2,1)} copy-done((bf16[1024,1024]{1,0:T(8,128)(2,1)}, bf16[1024,1024]{1,0:T(8,128)(2,1)S(1)}, u32[]{:S(2)}) %copy-start.4) | copy-done | bytes 2097176
  58.0 0.0 copy-start.6
  58.0 0.8 copy-done.6
  58.7 0.0 all-to-all-done
  58.7 0.0 copy-start.3
  58.7 1.6 %copy-done.3 = bf16[256,4096]{1,0:T(8,128)(2,1)S(1)} copy-done((bf16[256,4096]{1,0:T(8,128)(2,1)S(1)}, bf16[256,4096]{1,0:T(8,128)(2,1)}, u32[]{:S(2)}) %copy-start.3) | copy-done | bytes 2097176
  60.3 0.0 copy-start.5
  60.3 1.6 %copy-done.5 = bf16[1024,1024]{1,0:T(8,128)(2,1)S(1)} copy-done((bf16[1024,1024]{1,0:T(8,128)(2,1)S(1)}, bf16[1024,1024]{1,0:T(8,128)(2,1)}, u32[]{:S(2)}) %copy-start.5) | copy-done | bytes 2097176
  61.9 0.0 copy-start.7
  61.9 1.0 copy-done.7
  63.0 19.2 %radiate.1 = f32[256,2,128]{2,1,0:T(2,128)S(1)} custom-call(s32[32]{0:T(128)S(1)} %copy-done.1, bf16[4096,128]{1,0:T(8,128)(2,1)S(1)} %bitcast.11, f32[32,2,4,8,32,128]{5,4,3,2,1,0:T(8,128)} %get-tuple-element.11.waves_ref, f32[128,1024]{1,0:T(8,128)S(1)} %copy-done.7, bf16[8,128,1024]{2,1,0:T(8,128)(2,1)S(1)} %get-tuple-element.13.spread_ref, ...), custom_call_target="tpu_custom_call" | custom-call | flops 20000000000 | bytes 40000000 | tf_op jit(solution)/shard_map/radiate/pallas_call | solution.py:339
  82.1 30.4 %all_to_all.10.x_ref = f32[256,2,128]{2,1,0:T(2,128)} all-to-all(f32[256,2,128]{2,1,0:T(2,128)S(1)} %radiate.1), channel_id=1, replica_groups=mesh['panel'=64,'obs'=4] {'panel','obs'}, dimensions={0} | all-to-all | bytes 524288 | tf_op jit(solution)/shard_map/all_to_all | solution.py:402
  112.6 1.9 %gather.1 = f32[2,32,4]{2,1,0:T(8,128)} custom-call(f32[256,2,128]{2,1,0:T(2,128)} %all_to_all.10.x_ref), custom_call_target="tpu_custom_call" | custom-call | tf_op jit(solution)/shard_map/gather/pallas_call | solution.py:370
  114.5 1.4 %copy.14 = f32[2,32,4]{1,2,0:T(4,128)} copy(f32[2,32,4]{2,1,0:T(8,128)} %gather.1) | data formatting | bytes 2048 | tf_op jit(solution)/shard_map/gather/pallas_call | solution.py:370
  (1 shorter events, 0.0 us)
Async XLA Ops:
  0.0 21.0 %copy-start.8 = (f32[3,256]{1,0:T(4,128)S(1)}, f32[3,256]{1,0:T(4,128)}, u32[]{:S(2)}) copy-start(f32[3,256]{1,0:T(4,128)} %param.10) | copy-start | bytes 9220
  5.3 28.2 %copy-start.9 = (s32[4]{0:T(128)S(1)}, s32[4]{0:T(128)}, u32[]{:S(2)}) copy-start(s32[4]{0:T(128)} %param.9) | copy-start | bytes 52
  5.3 30.2 %copy-start = (f32[3,512]{1,0:T(4,128)S(1)}, f32[3,512]{1,0:T(4,128)}, u32[]{:S(2)}) copy-start(f32[3,512]{1,0:T(4,128)} %panel_ref.1) | copy-start | bytes 18436
  5.3 30.2 %copy-start.1 = (s32[32]{0:T(128)S(1)}, s32[32]{0:T(128)}, u32[]{:S(2)}) copy-start(s32[32]{0:T(128)} %bins_smem.3) | copy-start | bytes 388
  5.3 53.4 %all-to-all-start = ((bf16[256,4,4,128]{3,2,1,0:T(4,128)(2,1)}), bf16[256,4,4,128]{3,2,1,0:T(4,128)(2,1)S(1)}, u32[]{:S(2)}, u32[]{:S(2)}) async-start(bf16[256,4,4,128]{3,2,1,0:T(4,128)(2,1)} %arrange.1), calls=%async_computation | async-start | bytes 2097152 | tf_op jit(solution)/shard_map/all_to_all | solution.py:391
  55.2 1.3 %copy-start.2 = (bf16[256,4096]{1,0:T(8,128)(2,1)}, bf16[256,4096]{1,0:T(8,128)(2,1)S(1)}, u32[]{:S(2)}) copy-start(bf16[256,4096]{1,0:T(8,128)(2,1)S(1)} %get-tuple-element.14.table_ref) | copy-start | bytes 6291460
  56.6 1.4 %copy-start.4 = (bf16[1024,1024]{1,0:T(8,128)(2,1)}, bf16[1024,1024]{1,0:T(8,128)(2,1)S(1)}, u32[]{:S(2)}) copy-start(bf16[1024,1024]{1,0:T(8,128)(2,1)S(1)} %get-tuple-element.15.pick_ref) | copy-start | bytes 6291460
  58.0 0.8 copy-start.6
  58.7 1.6 %copy-start.3 = (bf16[256,4096]{1,0:T(8,128)(2,1)S(1)}, bf16[256,4096]{1,0:T(8,128)(2,1)}, u32[]{:S(2)}) copy-start(bf16[256,4096]{1,0:T(8,128)(2,1)} %copy-done.2) | copy-start | bytes 6291460
  60.3 1.6 %copy-start.5 = (bf16[1024,1024]{1,0:T(8,128)(2,1)S(1)}, bf16[1024,1024]{1,0:T(8,128)(2,1)}, u32[]{:S(2)}) copy-start(bf16[1024,1024]{1,0:T(8,128)(2,1)} %copy-done.4) | copy-start | bytes 6291460
  61.9 1.0 copy-start.7

commit v2 on v1

v2 whole, which is shorter than its diff:
```python
import math

import jax
import jax.numpy as jnp
from jax import lax
from jax.experimental import pallas as pl
from jax.experimental.pallas import tpu as pltpu
from jax.sharding import PartitionSpec as P


TIME = 1024
NF = 32
SPACING = 0.1
LANES = 128
CHANNELS = 4
AHEAD = 2
BLOCKS = 8
SLOTS = 4
TILE = 32
SLOT = 16

SIN_COEFFS = (
    4.442882919199695,
    -7.308245696158815,
    3.60635441147954,
    -0.8461128860931261,
    0.10982698817978952,
)
COS_COEFFS = (
    1.4142134965649862,
    -6.978850988235484,
    5.7394611706121585,
    -1.8835629868567052,
    0.31069819092073886,
)

VMEM = pl.BlockSpec(memory_space=pltpu.VMEM)
SMEM = pl.BlockSpec(memory_space=pltpu.SMEM)
HBM = pl.BlockSpec(memory_space=pltpu.HBM)


def horner(square, coeffs):
    total = square * coeffs[-1] + coeffs[-2]
    for coeff in coeffs[-3::-1]:
        total = total * square + coeff
    return total


def turn(cycles):
    part = cycles - jnp.round(cycles)
    square = part * part
    return part * horner(square, SIN_COEFFS), horner(square, COS_COEFFS)


def arrange_kernel(x_ref, o_ref, held_ref, sem):
    pieces, steps, _, piece = held_ref.shape
    copies = [
        pltpu.make_async_copy(x_ref.at[:, :, i * piece : (i + 1) * piece], held_ref.at[i], sem.at[i])
        for i in range(pieces)
    ]
    for copy in copies:
        copy.start()
    blocks = piece // LANES
    for i, copy in enumerate(copies):
        copy.wait()
        for block in range(blocks):
            for step in range(steps):
                o_ref[i * blocks + block, step] = held_ref[i, step, :, block * LANES : (block + 1) * LANES]


def arrange(samples):
    steps, channels, panels = samples.shape
    pieces = 4
    return pl.pallas_call(
        arrange_kernel,
        in_specs=[HBM],
        out_specs=VMEM,
        out_shape=jax.ShapeDtypeStruct((panels // LANES, steps, channels, LANES), samples.dtype),
        scratch_shapes=[
            pltpu.VMEM((pieces, steps, channels, panels // pieces), samples.dtype),
            pltpu.SemaphoreType.DMA((pieces,)),
        ],
        compiler_params=pltpu.CompilerParams(vmem_limit_bytes=8 << 20),
        name="arrange",
    )(pltpu.with_memory_space_constraint(samples, pltpu.HBM))


def bins_of_block(bins_smem, b):
    row = lax.broadcasted_iota(jnp.int32, (8, LANES), 0) % 4
    bins = [jnp.full((8, LANES), bins_smem[4 * b + i], jnp.int32) for i in range(4)]
    chosen = jnp.where(row == 0, bins[0], jnp.where(row == 1, bins[1], jnp.where(row == 2, bins[2], bins[3])))
    return chosen.astype(jnp.float32)


def wave_copy(held_ref, waves_ref, sem, slot, rows, lanes):
    return pltpu.make_async_copy(held_ref.at[slot], waves_ref.at[rows, lanes], sem.at[slot])


def prepare_kernel(
    bins_smem,
    place_smem,
    obs_ref,
    panel_ref,
    waves_ref,
    table_out_ref,
    column_ref,
    fine_ref,
    coarse_ref,
    held_ref,
    table_ref,
    sem,
    table_sem,
):
    start = pl.multiple_of(place_smem[0] * LANES, LANES)
    mine = panel_ref[:, pl.ds(start, LANES)]
    column_ref[...] = jnp.concatenate([mine, jnp.zeros((5, LANES), jnp.float32)], axis=0).T

    def one_chunk(chunk, carry):
        start = pl.multiple_of(chunk * LANES, LANES)
        time = ((lax.broadcasted_iota(jnp.int32, (8, LANES), 1) + start) >> 2).astype(jnp.float32)
        sine, cosine = turn(time * (1.0 / TIME))
        weight = (2.0 / TIME) * (0.5 * (sine * sine))
        is_real = lax.broadcasted_iota(jnp.int32, (8, LANES), 0) < 4
        values = []
        for b in range(BLOCKS):
            sine, cosine = turn(bins_of_block(bins_smem, b) * time * (1.0 / TIME))
            values.append(weight * jnp.where(is_real, 1.0 - sine * sine, -(sine * cosine)))
        table_ref[:, pl.ds(start, LANES)] = jnp.concatenate(values, axis=0).astype(jnp.bfloat16)
        return carry

    lax.fori_loop(0, TIME * CHANNELS // LANES, one_chunk, 0)
    table_copy = pltpu.make_async_copy(table_ref, table_out_ref, table_sem)
    table_copy.start()

    groups = obs_ref.shape[1] // LANES

    def one_tile(step, carry):
        row_tile, lane_tile, slot = step // groups, step % groups, step % SLOTS
        rows = pl.ds(pl.multiple_of(row_tile * TILE, TILE), TILE)
        lanes = pl.ds(pl.multiple_of(lane_tile * LANES, LANES), LANES)
        offsets = [obs_ref[c : c + 1, lanes] - column_ref[rows, c : c + 1] for c in range(3)]
        square = offsets[0] * offsets[0] + offsets[1] * offsets[1] + offsets[2] * offsets[2]
        inverse = lax.rsqrt(square)
        cycles = square * inverse * (1.0 / (TIME * SPACING))

        sine, cosine = turn(cycles)
        sines, cosines = sine * cosine, 1.0 - sine * sine
        double = cosines + cosines
        fine = [(inverse, jnp.zeros_like(inverse)), (inverse * cosines, inverse * sines)]
        for n in range(2, 17):
            fine.append(tuple(double * fine[n - 1][i] - fine[n - 2][i] for i in range(2)))
        for n in range(17):
            fine_ref[16 + n, 0] = fine[n][0]
            fine_ref[16 + n, 1] = fine[n][1]
            if n:
                fine_ref[16 - n, 0] = fine[n][0]
                fine_ref[16 - n, 1] = -fine[n][1]

        sine, cosine = turn(cycles * 32.0)
        coarse = [(jnp.ones_like(inverse), jnp.zeros_like(inverse)), (1.0 - sine * sine, sine * cosine)]
        for n in range(1, 9):
            twice = coarse[n][0] + coarse[n][0]
            coarse.append((twice * coarse[n][0] - 1.0, twice * coarse[n][1]))
            if n < 8:
                coarse.append(
                    (twice * coarse[n + 1][0] - coarse[1][0], twice * coarse[n + 1][1] - coarse[1][1])
                )
        for n in range(17):
            coarse_ref[n, 0] = coarse[n][0]
            coarse_ref[n, 1] = coarse[n][1]

        @pl.when(step >= SLOTS)
        def _():
            wave_copy(held_ref, waves_ref, sem, slot, 0, 0).wait()

        for j in range(NF):
            bin_number = bins_smem[j]
            whole = (bin_number + 16) >> 5
            rest = bin_number - (whole << 5) + 16
            c0, s0 = coarse_ref[whole, 0], coarse_ref[whole, 1]
            c1, s1 = fine_ref[rest, 0], fine_ref[rest, 1]
            held_ref[slot, j, 0] = (c0 * c1 - s0 * s1).astype(jnp.bfloat16)
            held_ref[slot, j, 1] = (s0 * c1 + c0 * s1).astype(jnp.bfloat16)
        wave_copy(held_ref, waves_ref, sem, slot, row_tile, lane_tile).start()
        return carry

    steps = (LANES // TILE) * groups
    lax.fori_loop(0, steps, one_tile, 0)

    for slot in range(SLOTS):
        wave_copy(held_ref, waves_ref, sem, slot, 0, 0).wait()
    table_copy.wait()


def prepare(bins, place, obs, panel_position):
    observers = obs.shape[1]
    f32 = jnp.float32
    return pl.pallas_call(
        prepare_kernel,
        in_specs=[SMEM, SMEM, VMEM, VMEM],
        out_specs=[HBM] * 2 + [VMEM],
        out_shape=[
            pltpu.HBM((LANES // TILE, observers // LANES, NF, 2, TILE, LANES), jnp.bfloat16),
            pltpu.HBM((2 * NF, CHANNELS * TIME), jnp.bfloat16),
            jax.ShapeDtypeStruct((LANES, 8), f32),
        ],
        scratch_shapes=[
            pltpu.VMEM((33, 2, TILE, LANES), f32),
            pltpu.VMEM((17, 2, TILE, LANES), f32),
            pltpu.VMEM((SLOTS, NF, 2, TILE, LANES), jnp.bfloat16),
            pltpu.VMEM((2 * NF, CHANNELS * TIME), jnp.bfloat16),
            pltpu.SemaphoreType.DMA((SLOTS,)),
            pltpu.SemaphoreType.DMA,
        ],
        cost_estimate=pl.CostEstimate(flops=20_000_000_000, bytes_accessed=40_000_000, transcendentals=0),
        compiler_params=pltpu.CompilerParams(vmem_limit_bytes=16 << 20),
        name="prepare",
    )(bins, place, obs, panel_position)


def wave_fetch(waves_ref, held_ref, sem, b):
    return pltpu.make_async_copy(waves_ref.at[:, :, pl.ds(b * 4, 4)], held_ref.at[b], sem.at[b])


def radiate_kernel(
    bins_smem,
    data_ref,
    obs_ref,
    waves_ref,
    table_in_ref,
    column_ref,
    scale_ref,
    o_ref,
    left_ref,
    mono_ref,
    product_ref,
    field_ref,
    inverse_ref,
    spread_ref,
    pick_ref,
    narrow_ref,
    table_ref,
    held_ref,
    sem,
    table_sem,
):
    table_copy = pltpu.make_async_copy(table_in_ref, narrow_ref, table_sem)
    table_copy.start()
    rows = 2 * NF

    obs = obs_ref[...]
    high = obs.astype(jnp.bfloat16).astype(jnp.float32)
    low = obs - high
    minus = jnp.full((6, obs.shape[1]), -1.0, jnp.float32)
    slot_rows = jnp.concatenate([high, high, low, minus, jnp.zeros((1, obs.shape[1]), jnp.float32)], axis=0)
    spread_ref[...] = jnp.zeros_like(spread_ref)
    for s in range(8):
        spread_ref[s, s * SLOT : (s + 1) * SLOT, :] = slot_rows.astype(jnp.bfloat16)

    for group in range(obs_ref.shape[1] // LANES):
        lanes = slice(group * LANES, (group + 1) * LANES)
        offsets = [obs_ref[c : c + 1, lanes] - column_ref[:, c : c + 1] for c in range(3)]
        square = offsets[0] * offsets[0] + offsets[1] * offsets[1] + offsets[2] * offsets[2]
        inverse_ref[:, lanes] = lax.rsqrt(square)

    source = lax.broadcasted_iota(jnp.int32, (rows, pick_ref.shape[1]), 0)
    target = lax.broadcasted_iota(jnp.int32, (rows, pick_ref.shape[1]), 1)
    same = jnp.where((target >> 4) == source, 1.0, 0.0)
    slot = lax.broadcasted_iota(jnp.int32, (8, pick_ref.shape[1]), 1) & 15
    for piece, bases in enumerate(((0, 6), (3, 3), (9, 9), (12, 12))):
        for direction in range(4):
            first = piece * 256 + direction * rows
            if direction == 3:
                pick_ref[first : first + rows, :] = jnp.zeros((rows, pick_ref.shape[1]), jnp.bfloat16)
                continue
            match = (slot == bases[0] + direction) | (slot == bases[1] + direction)
            chosen = jnp.where(match, 1.0, 0.0)
            pick_ref[first : first + rows, :] = (same * chosen[0:1]).astype(jnp.bfloat16)

    channel = lax.broadcasted_iota(jnp.int32, (16, LANES), 1) & 3
    table_copy.wait()
    for b in range(AHEAD):
        wave_fetch(waves_ref, held_ref, sem, b).start()
    for c in range(CHANNELS):
        mask = jnp.where(channel == (c + 1) % CHANNELS, 1.0, 0.0).astype(jnp.bfloat16)[0:1]
        for chunk in range(CHANNELS * TIME // LANES):
            lanes = slice(chunk * LANES, (chunk + 1) * LANES)
            table_ref[c * rows : (c + 1) * rows, lanes] = narrow_ref[:, lanes] * mask
    spectra = jnp.dot(table_ref[...], data_ref[...], preferred_element_type=jnp.float32)
    scales = [
        bins_of_block(bins_smem, b) * (2.0 * math.pi / (TIME * SPACING)) * scale_ref[...] for b in range(BLOCKS)
    ]
    turned = (spectra * jnp.concatenate(scales * CHANNELS, axis=0)).T
    lane = lax.broadcasted_iota(jnp.int32, turned.shape, 1)
    position = jnp.where(
        lane < 64, column_ref[:, 0:1], jnp.where(lane < 128, column_ref[:, 1:2], column_ref[:, 2:3])
    )
    moment = turned * position
    high = turned.astype(jnp.bfloat16)
    low = (turned - high.astype(jnp.float32)).astype(jnp.bfloat16)
    moment_high = moment.astype(jnp.bfloat16)
    moment_low = (moment - moment_high.astype(jnp.float32)).astype(jnp.bfloat16)
    pieces = jnp.concatenate([high, low, moment_high, moment_low], axis=1)
    slots = jnp.dot(pieces, pick_ref[...], preferred_element_type=jnp.float32).astype(jnp.bfloat16)
    for b in range(BLOCKS):
        left_ref[b] = slots[:, b * LANES : (b + 1) * LANES]
        mono_ref[b, :, 0:8] = turned[:, 192 + 8 * b : 200 + 8 * b]

    panels = inverse_ref.shape[0]
    width = 256

    def one_block(b, carry):
        @pl.when(b + AHEAD < BLOCKS)
        def _():
            wave_fetch(waves_ref, held_ref, sem, b + AHEAD).start()

        left = left_ref[b]
        wave_fetch(waves_ref, held_ref, sem, b).wait()
        for jj in range(4):
            j = b * 4 + jj
            wave = jnp.full((8, LANES), bins_smem[j], jnp.int32).astype(jnp.float32)
            inverse_wave = 1.0 / (wave * (2.0 * math.pi / (TIME * SPACING)))
            mono_real = jnp.broadcast_to(mono_ref[b, :, jj : jj + 1], (panels, LANES))
            mono_imag = jnp.broadcast_to(mono_ref[b, :, 4 + jj : 5 + jj], (panels, LANES))
            for t in range(inverse_ref.shape[1] // width):
                parity = t % 2
                columns = slice(t * width, (t + 1) * width)
                product_ref[parity, 0] = jnp.dot(
                    left, spread_ref[jj, :, columns], preferred_element_type=jnp.float32
                )
                product_ref[parity, 1] = jnp.dot(
                    left, spread_ref[4 + jj, :, columns], preferred_element_type=jnp.float32
                )
                for half in range(2):
                    inner = slice(half * LANES, (half + 1) * LANES)
                    lane_tile = t * 2 + half
                    lanes = slice(lane_tile * LANES, (lane_tile + 1) * LANES)
                    sum_real = jnp.zeros((8, LANES), jnp.float32)
                    sum_imag = jnp.zeros((8, LANES), jnp.float32)
                    for p in range(panels // 8):
                        rows = slice(p * 8, p * 8 + 8)
                        inverse = inverse_ref[rows, lanes]
                        if p % 2 == 0:
                            row_tile, inside = p * 8 // TILE, slice(p * 8 % TILE, p * 8 % TILE + 16)
                            cosines = held_ref[b, row_tile, lane_tile, jj, 0, inside].astype(jnp.float32)
                            sines = held_ref[b, row_tile, lane_tile, jj, 1, inside].astype(jnp.float32)
                        cosine = cosines[p % 2 * 8 : p % 2 * 8 + 8]
                        sine = sines[p % 2 * 8 : p % 2 * 8 + 8]
                        radial_real = product_ref[parity, 0, rows, inner] * inverse
                        radial_imag = product_ref[parity, 1, rows, inner] * inverse
                        near = inverse * inverse_wave
                        source_real = near * radial_real - (mono_imag[rows] + radial_imag)
                        source_imag = near * radial_imag + (mono_real[rows] + radial_real)
                        sum_real = sum_real + (cosine * source_real + sine * source_imag)
                        sum_imag = sum_imag + (cosine * source_imag - sine * source_real)
                    row = t * 4 + jj
                    field_ref[b, 0, row : row + 1, inner] = jnp.sum(sum_real, axis=0, keepdims=True)
                    field_ref[b, 1, row : row + 1, inner] = jnp.sum(sum_imag, axis=0, keepdims=True)
        return carry

    lax.fori_loop(0, BLOCKS, one_block, 0)
    for part in range(2):
        flat = jnp.concatenate(
            [field_ref[b, part, 4 * t : 4 * t + 4] for t in range(4) for b in range(BLOCKS)], axis=0
        )
        o_ref[:, part, :] = flat.T


def radiate(bins, data, observers, prepared, scale):
    panels, count = LANES, observers.shape[1]
    return pl.pallas_call(
        radiate_kernel,
        in_specs=[SMEM, VMEM, VMEM, HBM, HBM, VMEM, VMEM],
        out_specs=VMEM,
        out_shape=jax.ShapeDtypeStruct((count // 4, 2, LANES), jnp.float32),
        scratch_shapes=[
            pltpu.VMEM((BLOCKS, panels, LANES), jnp.bfloat16),
            pltpu.VMEM((BLOCKS, panels, LANES), jnp.float32),
            pltpu.VMEM((2, 2, panels, 256), jnp.float32),
            pltpu.VMEM((BLOCKS, 2, 16, 256), jnp.float32),
            pltpu.VMEM((panels, count), jnp.float32),
            pltpu.VMEM((8, LANES, count), jnp.bfloat16),
            pltpu.VMEM((1024, 1024), jnp.bfloat16),
            pltpu.VMEM((2 * NF, CHANNELS * TIME), jnp.bfloat16),
            pltpu.VMEM((CHANNELS * 2 * NF, CHANNELS * TIME), jnp.bfloat16),
            pltpu.VMEM((BLOCKS, panels // TILE, count // LANES, 4, 2, TILE, LANES), jnp.bfloat16),
            pltpu.SemaphoreType.DMA((BLOCKS,)),
            pltpu.SemaphoreType.DMA,
        ],
        cost_estimate=pl.CostEstimate(flops=20_000_000_000, bytes_accessed=40_000_000, transcendentals=0),
        compiler_params=pltpu.CompilerParams(vmem_limit_bytes=40 << 20),
        name="radiate",
    )(bins, data, observers, *prepared, scale)


def gather_kernel(x_ref, o_ref):
    total = jnp.sum(x_ref[...], axis=0)
    for part in range(2):
        for i in range(4):
            o_ref[part, i : i + 1, :] = total[part : part + 1, i * NF : (i + 1) * NF]


def gather(arrived):
    return pl.pallas_call(
        gather_kernel,
        in_specs=[VMEM],
        out_specs=VMEM,
        out_shape=jax.ShapeDtypeStruct((2, 4, NF), jnp.float32),
        name="gather",
    )(arrived)


def all_observers(obs_position):
    size = lax.axis_size("obs")
    local = jnp.transpose(obs_position.reshape(3, -1, 4), (0, 2, 1)).reshape(12, -1)
    held = [local]
    for shift in range(1, size):
        held.append(lax.ppermute(local, "obs", [((i + shift) % size, i) for i in range(size)]))
    own = lax.axis_index("obs")
    ring = jnp.stack(held + held)
    whole = lax.dynamic_slice_in_dim(ring, (size - own) % size, size, 0)
    return jnp.transpose(whole, (1, 2, 0)).reshape(3, -1)


def local_field(data, place, panel_position, scale, observers, bins):
    prepared = prepare(bins, place, observers, panel_position)
    waves, table, columns = prepared
    held = [pltpu.with_memory_space_constraint(v, pltpu.HBM) for v in (waves, table)]
    return radiate(bins, data, observers, (*held, columns), scale)


def shards(samples, panel_position, panel_area, panel_counts, obs_position, freq_bins):
    arrived = lax.all_to_all(arrange(samples), ("panel", "obs"), 0, 0, tiled=True)
    data = arrived.reshape(-1, LANES)
    observers = all_observers(obs_position)

    place = lax.axis_index("obs")
    area = lax.dynamic_slice_in_dim(panel_area, place * LANES, LANES, 0)
    count = lax.dynamic_slice_in_dim(panel_counts, place, 1, 0)
    lane_ids = jnp.arange(LANES, dtype=jnp.int32)
    scale = jnp.where(lane_ids < count, area * (1.0 / (4.0 * math.pi)), 0.0)[None, :]

    partial = local_field(data, place.reshape(1), panel_position, scale, observers, freq_bins)
    arrived = lax.all_to_all(partial, ("panel", "obs"), 0, 0, tiled=True)
    return jnp.transpose(gather(arrived), (0, 2, 1))


def solution(mesh):
    in_specs = (
        P(("panel", "obs"), None, None),
        P(None, "panel"),
        P("panel"),
        P("panel"),
        P(None, "obs"),
        P(),
    )
    out_specs = P(None, None, ("obs", "panel"))
    return jax.shard_map(shards, mesh=mesh, in_specs=in_specs, out_specs=out_specs, check_vma=False)
```

time: 116 us -> 95.4 us (0.82)
  blocking collectives: 40.8 us -> 21.8 us
  waiting for transfers between devices: 0.01 us -> 10 us
  local copies, waits for them, and re-layouts: 11.9 us -> 4.05 us
  Pallas kernels: 46.1 us -> 38.6 us
  starting transfers between devices: 15.6 us -> 19 us
    all_gather x1 -> x0, blocking collectives: 10.4 us -> none  [all_observers(): whole = lax.all_gather(obs_position, 'obs')]
    all_to_all x1, waiting for transfers between devices: 0.01 us -> 9.99 us  [shards(): lax.all_to_all(arrange(samples), ('panel', 'obs'), 0, 0, tiled=True)]
    all_to_all x1, blocking collectives: 30.4 us -> 21.8 us  [shards(): arrived = lax.all_to_all(partial, ('panel', 'obs'), 0, 0, tiled=True)]
    unnamed x20 -> x13, local copies, waits for them, and re-layouts: 7.74 us -> 1.37 us
    ppermute x0 -> x3, starting transfers between devices: none -> 5.88 us  [all_observers(): lax.ppermute(local, 'obs', [((i + shift) % size, i) for i in range(size)])]
    pallas_call x2, Pallas kernels: 24.5 us -> 20.5 us  [the longest x1 18.2 us: radiate(): pl.pallas_call(radiate_kernel, in_specs=[SMEM, VMEM, VMEM, HBM, HBM, VMEM...]
    pallas_call x1, Pallas kernels: 19.7 us -> 16.2 us  [prepare(): pl.pallas_call(prepare_kernel, in_specs=[SMEM, SMEM, VMEM, VMEM], out_spe...]
    all_to_all x1, starting transfers between devices: 15.6 us -> 13.2 us  [shards(): lax.all_to_all(arrange(samples), ('panel', 'obs'), 0, 0, tiled=True)]
  transfers between devices with their start and end apart: 1 -> 4, of which waited for: 0 -> 1; matrix products, arithmetic and copies ran while one was open for 4% -> 3% of each run, Pallas kernels for 17% -> 19%
where the time goes in v2:
time: 95.4 us; the launch traced here: 95 us
  Pallas kernels  38.6 us (40%)
  blocking collectives  21.8 us (23%)
  starting transfers between devices  19 us (20%)
  waiting for transfers between devices  10 us (10%)
  local copies, waits for them, and re-layouts  4.05 us (4%)
  other arithmetic  1.44 us (2%)
    all_to_all x1, blocking collectives, shards(): arrived = lax.all_to_all(partial, ('panel', 'obs'), 0, 0, tiled=True)  21.8 us
    pallas_call x1, Pallas kernels, radiate(): pl.pallas_call(radiate_kernel, in_specs=[SMEM, VMEM, VMEM, HBM, HBM, VMEM...  18.2 us
    pallas_call x1, Pallas kernels, prepare(): pl.pallas_call(prepare_kernel, in_specs=[SMEM, SMEM, VMEM, VMEM], out_spe...  16.2 us
    all_to_all x1, starting transfers between devices, shards(): lax.all_to_all(arrange(samples), ('panel', 'obs'), 0, 0, tiled=True)  13.2 us
    all_to_all x1, waiting for transfers between devices, shards(): lax.all_to_all(arrange(samples), ('panel', 'obs'), 0, 0, tiled=True)  9.99 us
    ppermute x3, starting transfers between devices, all_observers(): lax.ppermute(local, 'obs', [((i + shift) % size, i) for i in range(size)])  5.88 us
    pallas_call x1, Pallas kernels, arrange(): pl.pallas_call(arrange_kernel, in_specs=[HBM], out_specs=VMEM, out_shape=...  2.33 us
  transfers between devices with their start and end apart: 4, of which 1 were waited for; matrix products, arithmetic and copies ran while one was open for 3% of the time, Pallas kernels for 19%

profile of v2, /device:TPU:1, one launch (start us, length us, event | category | flops | bytes accessed | tf_op | source)
XLA Modules:
  0.0 95.0 jit_solution(7044156551280545576)
XLA Ops:
  0.0 0.8 reshape.16
  0.8 0.1 copy.15
  0.9 2.2 %collective-permute-start.2 = (f32[12,64]{1,0:T(8,128)S(1)}, f32[12,64]{1,0:T(8,128)S(1)}, u32[]{:S(2)}, u32[]{:S(2)}) collective-permute-start(f32[12,64]{1,0:T(8,128)S(1)} %reshape.17), channel_id=1, source_target_pairs={{3,0},{0,1},{1,2},{2,3},{7,4},{4,5},{5,6},{6,7},{11,8},{8,9},{9,10... | collective-permute-start | bytes 9224 | tf_op jit(solution)/shard_map/ppermute | solution.py:418
  3.1 2.6 %collective-permute-start.1 = (f32[12,64]{1,0:T(8,128)S(1)}, f32[12,64]{1,0:T(8,128)S(1)}, u32[]{:S(2)}, u32[]{:S(2)}) collective-permute-start(f32[12,64]{1,0:T(8,128)S(1)} %reshape.17), channel_id=1, source_target_pairs={{2,0},{3,1},{0,2},{1,3},{6,4},{7,5},{4,6},{5,7},{10,8},{11,9},{8,1... | collective-permute-start | bytes 9224 | tf_op jit(solution)/shard_map/ppermute | solution.py:418
  5.7 1.1 %collective-permute-start = (f32[12,64]{1,0:T(8,128)S(1)}, f32[12,64]{1,0:T(8,128)S(1)}, u32[]{:S(2)}, u32[]{:S(2)}) collective-permute-start(f32[12,64]{1,0:T(8,128)S(1)} %reshape.17), channel_id=1, source_target_pairs={{1,0},{2,1},{3,2},{0,3},{5,4},{6,5},{7,6},{4,7},{9,8},{10,9},{11,1... | collective-permute-start | bytes 9224 | tf_op jit(solution)/shard_map/ppermute | solution.py:418
  6.8 2.3 %arrange.1 = bf16[256,4,4,128]{3,2,1,0:T(4,128)(2,1)} custom-call(bf16[4,4,32768]{2,1,0:T(4,128)(2,1)} %x_ref.1), custom_call_target="tpu_custom_call" | custom-call | tf_op jit(solution)/shard_map/arrange/pallas_call | solution.py:74
  9.1 13.2 %all-to-all-start = ((bf16[256,4,4,128]{3,2,1,0:T(4,128)(2,1)}), bf16[256,4,4,128]{3,2,1,0:T(4,128)(2,1)S(1)}, u32[]{:S(2)}, u32[]{:S(2)}) async-start(bf16[256,4,4,128]{3,2,1,0:T(4,128)(2,1)} %arrange.1), calls=%async_computation | async-start | bytes 2097152 | tf_op jit(solution)/shard_map/all_to_all | solution.py:433
  22.3 1.3 %dynamic_slice.10 = s32[1]{0:T(128)} dynamic-slice(s32[4]{0:T(128)} %param.9, s32[]{:T(128)S(6)} %select_n.22), dynamic_slice_sizes={1} | dynamic-slice | bytes 12 | tf_op jit(solution)/shard_map/dynamic_slice | solution.py:439
  23.6 1.4 %fusion.scale_ref = f32[1,128]{1,0:T(1,128)S(1)} fusion(f32[512]{0:T(512)} %param.8, s32[]{:T(128)S(6)} %select_n.23, s32[]{:T(128)} %bitcast.7), kind=kLoop, calls=%fused_computation.10 | loop fusion | flops 384 | bytes 1032 | tf_op jit(solution)/shard_map/broadcast_in_dim | solution.py:441
  25.1 0.0 collective-permute-done
  25.1 0.0 collective-permute-done.1
  25.1 0.0 collective-permute-done.2
  25.2 0.2 copy.17
  25.4 0.2 reshape.18.obs_ref
  25.6 0.0 copy-start
  25.6 0.7 copy-done
  26.3 0.0 copy-start.1
  26.3 0.7 copy-done.1
  27.0 0.0 copy-start.2
  27.0 16.2 %prepare.1 = (bf16[4,8,32,2,32,128]{5,4,3,2,1,0:T(8,128)(2,1)}, bf16[64,4096]{1,0:T(8,128)(2,1)}, f32[128,8]{1,0:T(8,128)S(1)}) custom-call(s32[32]{0:T(128)S(1)} %copy-done.1, s32[1]{0:T(128)} %bitcast.6.place_smem, f32[3,1024]{1,0:T(4,128)S(1)} %reshape.18.obs_ref, f32[3,512]{1,0:T(4,128)S(1)} %copy-done), custom_call_target="tpu_custom_call" | custom-call | flops 20000000000 | bytes 40000000 | tf_op jit(solution)/shard_map/prepare/pallas_call | solution.py:198
  43.2 10.0 %all-to-all-done = bf16[256,4,4,128]{3,2,1,0:T(4,128)(2,1)S(1)} async-done(((bf16[256,4,4,128]{3,2,1,0:T(4,128)(2,1)}), bf16[256,4,4,128]{3,2,1,0:T(4,128)(2,1)S(1)}, u32[]{:S(2)}, u32[]{:S(2)}) %all-to-all-start) | async-done | bytes 1048608 | tf_op jit(solution)/shard_map/all_to_all | solution.py:433
  53.1 0.0 copy-done.2
  53.1 18.2 %radiate.1 = f32[256,2,128]{2,1,0:T(2,128)S(1)} custom-call(s32[32]{0:T(128)S(1)} %copy-done.2, bf16[4096,128]{1,0:T(8,128)(2,1)S(1)} %bitcast.18, f32[3,1024]{1,0:T(4,128)S(1)} %reshape.18.obs_ref, bf16[4,8,32,2,32,128]{5,4,3,2,1,0:T(8,128)(2,1)} %get-tuple-element.8.waves_ref, bf16[64,4096]{1,0:T(8,128)(2,1)} %get-tuple-element.9.table_in_ref, ...), custom_call_target="tpu_custom_call" | custom-call | flops 20000000000 | bytes 40000000 | tf_op jit(solution)/shard_map/radiate/pallas_call | solution.py:371
  71.4 21.8 %all_to_all.10.x_ref = f32[256,2,128]{2,1,0:T(2,128)} all-to-all(f32[256,2,128]{2,1,0:T(2,128)S(1)} %radiate.1), channel_id=1, replica_groups=mesh['panel'=64,'obs'=4] {'panel','obs'}, dimensions={0} | all-to-all | bytes 524288 | tf_op jit(solution)/shard_map/all_to_all | solution.py:444
  93.1 1.9 %gather.1 = f32[2,4,32]{2,1,0:T(4,128)} custom-call(f32[256,2,128]{2,1,0:T(2,128)} %all_to_all.10.x_ref), custom_call_target="tpu_custom_call" | custom-call | tf_op jit(solution)/shard_map/gather/pallas_call | solution.py:404
  (11 shorter events, 0.1 us)
Async XLA Ops:
  0.9 24.2 %collective-permute-start.2 = (f32[12,64]{1,0:T(8,128)S(1)}, f32[12,64]{1,0:T(8,128)S(1)}, u32[]{:S(2)}, u32[]{:S(2)}) collective-permute-start(f32[12,64]{1,0:T(8,128)S(1)} %reshape.17), channel_id=1, source_target_pairs={{3,0},{0,1},{1,2},{2,3},{7,4},{4,5},{5,6},{6,7},{11,8},{8,9},{9,10... | collective-permute-start | bytes 9224 | tf_op jit(solution)/shard_map/ppermute | solution.py:418
  3.1 22.0 %collective-permute-start.1 = (f32[12,64]{1,0:T(8,128)S(1)}, f32[12,64]{1,0:T(8,128)S(1)}, u32[]{:S(2)}, u32[]{:S(2)}) collective-permute-start(f32[12,64]{1,0:T(8,128)S(1)} %reshape.17), channel_id=1, source_target_pairs={{2,0},{3,1},{0,2},{1,3},{6,4},{7,5},{4,6},{5,7},{10,8},{11,9},{8,1... | collective-permute-start | bytes 9224 | tf_op jit(solution)/shard_map/ppermute | solution.py:418
  5.7 19.4 %collective-permute-start = (f32[12,64]{1,0:T(8,128)S(1)}, f32[12,64]{1,0:T(8,128)S(1)}, u32[]{:S(2)}, u32[]{:S(2)}) collective-permute-start(f32[12,64]{1,0:T(8,128)S(1)} %reshape.17), channel_id=1, source_target_pairs={{1,0},{2,1},{3,2},{0,3},{5,4},{6,5},{7,6},{4,7},{9,8},{10,9},{11,1... | collective-permute-start | bytes 9224 | tf_op jit(solution)/shard_map/ppermute | solution.py:418
  9.1 44.0 %all-to-all-start = ((bf16[256,4,4,128]{3,2,1,0:T(4,128)(2,1)}), bf16[256,4,4,128]{3,2,1,0:T(4,128)(2,1)S(1)}, u32[]{:S(2)}, u32[]{:S(2)}) async-start(bf16[256,4,4,128]{3,2,1,0:T(4,128)(2,1)} %arrange.1), calls=%async_computation | async-start | bytes 2097152 | tf_op jit(solution)/shard_map/all_to_all | solution.py:433
  25.6 0.7 copy-start
  26.3 0.7 copy-start.1
  27.0 26.2 %copy-start.2 = (s32[32]{0:T(128)S(1)}, s32[32]{0:T(128)}, u32[]{:S(2)}) copy-start(s32[32]{0:T(128)} %bins_smem.3) | copy-start | bytes 388

commit v3 on v2

--- a/solution.py
+++ b/solution.py
@@ -13,11 +13,10 @@
 SPACING = 0.1
 LANES = 128
 CHANNELS = 4
-AHEAD = 2
+AHEAD = 3
 BLOCKS = 8
 SLOTS = 4
 TILE = 32
-SLOT = 16
 
 SIN_COEFFS = (
     4.442882919199695,
@@ -104,6 +103,7 @@
     waves_ref,
     table_out_ref,
     column_ref,
+    position_ref,
     fine_ref,
     coarse_ref,
     held_ref,
@@ -113,7 +113,8 @@
 ):
     start = pl.multiple_of(place_smem[0] * LANES, LANES)
     mine = panel_ref[:, pl.ds(start, LANES)]
-    column_ref[...] = jnp.concatenate([mine, jnp.zeros((5, LANES), jnp.float32)], axis=0).T
+    position_ref[...] = jnp.concatenate([mine, jnp.zeros((5, LANES), jnp.float32)], axis=0)
+    column_ref[...] = position_ref[...].T
 
     def one_chunk(chunk, carry):
         start = pl.multiple_of(chunk * LANES, LANES)
@@ -198,11 +199,12 @@
     return pl.pallas_call(
         prepare_kernel,
         in_specs=[SMEM, SMEM, VMEM, VMEM],
-        out_specs=[HBM] * 2 + [VMEM],
+        out_specs=[HBM] * 2 + [VMEM] * 2,
         out_shape=[
             pltpu.HBM((LANES // TILE, observers // LANES, NF, 2, TILE, LANES), jnp.bfloat16),
             pltpu.HBM((2 * NF, CHANNELS * TIME), jnp.bfloat16),
             jax.ShapeDtypeStruct((LANES, 8), f32),
+            jax.ShapeDtypeStruct((8, LANES), f32),
         ],
         scratch_shapes=[
             pltpu.VMEM((33, 2, TILE, LANES), f32),
@@ -224,87 +226,82 @@
 
 def radiate_kernel(
     bins_smem,
-    data_ref,
+    data_in_ref,
     obs_ref,
     waves_ref,
     table_in_ref,
     column_ref,
+    position_ref,
     scale_ref,
     o_ref,
     left_ref,
-    mono_ref,
     product_ref,
     field_ref,
     inverse_ref,
     spread_ref,
-    pick_ref,
     narrow_ref,
     table_ref,
+    data_ref,
+    source_ref,
     held_ref,
     sem,
-    table_sem,
+    in_sem,
 ):
-    table_copy = pltpu.make_async_copy(table_in_ref, narrow_ref, table_sem)
+    table_copy = pltpu.make_async_copy(table_in_ref, narrow_ref, in_sem.at[0])
     table_copy.start()
+    data_copy = pltpu.make_async_copy(data_in_ref, data_ref, in_sem.at[1])
+    data_copy.start()
+    for b in range(AHEAD):
+        wave_fetch(waves_ref, held_ref, sem, b).start()
     rows = 2 * NF
 
     obs = obs_ref[...]
     high = obs.astype(jnp.bfloat16).astype(jnp.float32)
     low = obs - high
-    minus = jnp.full((6, obs.shape[1]), -1.0, jnp.float32)
-    slot_rows = jnp.concatenate([high, high, low, minus, jnp.zeros((1, obs.shape[1]), jnp.float32)], axis=0)
-    spread_ref[...] = jnp.zeros_like(spread_ref)
-    for s in range(8):
-        spread_ref[s, s * SLOT : (s + 1) * SLOT, :] = slot_rows.astype(jnp.bfloat16)
-
+    minus = jnp.full((1, obs.shape[1]), -1.0, jnp.float32)
+    factors = [v[c : c + 1] for v in (high, high, low) for c in range(3)] + [minus] * 6 + [minus * 0.0]
+    spread_ref[...] = jnp.concatenate(
+        [jnp.broadcast_to(v, (8, obs.shape[1])) for v in factors], axis=0
+    ).astype(jnp.bfloat16)
     for group in range(obs_ref.shape[1] // LANES):
         lanes = slice(group * LANES, (group + 1) * LANES)
         offsets = [obs_ref[c : c + 1, lanes] - column_ref[:, c : c + 1] for c in range(3)]
         square = offsets[0] * offsets[0] + offsets[1] * offsets[1] + offsets[2] * offsets[2]
         inverse_ref[:, lanes] = lax.rsqrt(square)
 
-    source = lax.broadcasted_iota(jnp.int32, (rows, pick_ref.shape[1]), 0)
-    target = lax.broadcasted_iota(jnp.int32, (rows, pick_ref.shape[1]), 1)
-    same = jnp.where((target >> 4) == source, 1.0, 0.0)
-    slot = lax.broadcasted_iota(jnp.int32, (8, pick_ref.shape[1]), 1) & 15
-    for piece, bases in enumerate(((0, 6), (3, 3), (9, 9), (12, 12))):
-        for direction in range(4):
-            first = piece * 256 + direction * rows
-            if direction == 3:
-                pick_ref[first : first + rows, :] = jnp.zeros((rows, pick_ref.shape[1]), jnp.bfloat16)
-                continue
-            match = (slot == bases[0] + direction) | (slot == bases[1] + direction)
-            chosen = jnp.where(match, 1.0, 0.0)
-            pick_ref[first : first + rows, :] = (same * chosen[0:1]).astype(jnp.bfloat16)
-
     channel = lax.broadcasted_iota(jnp.int32, (16, LANES), 1) & 3
     table_copy.wait()
-    for b in range(AHEAD):
-        wave_fetch(waves_ref, held_ref, sem, b).start()
     for c in range(CHANNELS):
         mask = jnp.where(channel == (c + 1) % CHANNELS, 1.0, 0.0).astype(jnp.bfloat16)[0:1]
         for chunk in range(CHANNELS * TIME // LANES):
             lanes = slice(chunk * LANES, (chunk + 1) * LANES)
             table_ref[c * rows : (c + 1) * rows, lanes] = narrow_ref[:, lanes] * mask
+    data_copy.wait()
     spectra = jnp.dot(table_ref[...], data_ref[...], preferred_element_type=jnp.float32)
     scales = [
         bins_of_block(bins_smem, b) * (2.0 * math.pi / (TIME * SPACING)) * scale_ref[...] for b in range(BLOCKS)
     ]
-    turned = (spectra * jnp.concatenate(scales * CHANNELS, axis=0)).T
-    lane = lax.broadcasted_iota(jnp.int32, turned.shape, 1)
-    position = jnp.where(
-        lane < 64, column_ref[:, 0:1], jnp.where(lane < 128, column_ref[:, 1:2], column_ref[:, 2:3])
-    )
-    moment = turned * position
-    high = turned.astype(jnp.bfloat16)
-    low = (turned - high.astype(jnp.float32)).astype(jnp.bfloat16)
-    moment_high = moment.astype(jnp.bfloat16)
-    moment_low = (moment - moment_high.astype(jnp.float32)).astype(jnp.bfloat16)
-    pieces = jnp.concatenate([high, low, moment_high, moment_low], axis=1)
-    slots = jnp.dot(pieces, pick_ref[...], preferred_element_type=jnp.float32).astype(jnp.bfloat16)
+    spectra = spectra * jnp.concatenate(scales * CHANNELS, axis=0)
+    row = lax.broadcasted_iota(jnp.int32, (8, LANES), 0)
+    blank = jnp.zeros((8, 2 * LANES), jnp.float32)
     for b in range(BLOCKS):
-        left_ref[b] = slots[:, b * LANES : (b + 1) * LANES]
-        mono_ref[b, :, 0:8] = turned[:, 192 + 8 * b : 200 + 8 * b]
+        whole = spectra[192 + 8 * b : 200 + 8 * b]
+        lead = whole.astype(jnp.bfloat16).astype(jnp.float32)
+        rest = whole - lead
+        for jj in range(4):
+            real = jnp.where(row < 2, lead[jj : jj + 1], rest[jj : jj + 1])
+            imag = jnp.where(row < 2, lead[4 + jj : 5 + jj], rest[4 + jj : 5 + jj])
+            by_cosine = jnp.where(row % 2 == 0, -imag, real)
+            by_sine = jnp.where(row % 2 == 0, real, imag)
+            both = jnp.where(lax.broadcasted_iota(jnp.int32, (8, 2 * LANES), 0) < 4, jnp.concatenate([by_cosine, by_sine], axis=1), 0.0)
+            source_ref[4 * b + jj] = jnp.concatenate([both, blank], axis=0).astype(jnp.bfloat16)
+    for b in range(BLOCKS):
+        direct = [spectra[c * rows + 8 * b : c * rows + 8 * b + 8] for c in range(3)]
+        moment = [direct[c] * position_ref[c : c + 1, :] for c in range(3)]
+        lead = [v.astype(jnp.bfloat16).astype(jnp.float32) for v in direct + moment]
+        rest = [v - w for v, w in zip(direct + moment, lead)]
+        slots = lead[:3] + rest[:3] + lead[:3] + lead[3:] + rest[3:] + [jnp.zeros((8, LANES), jnp.float32)]
+        left_ref[b] = jnp.concatenate(slots, axis=0).T.astype(jnp.bfloat16)
 
     panels = inverse_ref.shape[0]
     width = 256
@@ -315,28 +312,37 @@
             wave_fetch(waves_ref, held_ref, sem, b + AHEAD).start()
 
         left = left_ref[b]
+        lane = lax.broadcasted_iota(jnp.int32, (16, LANES), 1) & 7
         wave_fetch(waves_ref, held_ref, sem, b).wait()
         for jj in range(4):
             j = b * 4 + jj
             wave = jnp.full((8, LANES), bins_smem[j], jnp.int32).astype(jnp.float32)
             inverse_wave = 1.0 / (wave * (2.0 * math.pi / (TIME * SPACING)))
-            mono_real = jnp.broadcast_to(mono_ref[b, :, jj : jj + 1], (panels, LANES))
-            mono_imag = jnp.broadcast_to(mono_ref[b, :, 4 + jj : 5 + jj], (panels, LANES))
+            source = source_ref[j]
+            parts = [
+                left * jnp.where(lane == s, 1.0, 0.0).astype(jnp.bfloat16)[0:1] for s in (jj, 4 + jj)
+            ]
             for t in range(inverse_ref.shape[1] // width):
                 parity = t % 2
                 columns = slice(t * width, (t + 1) * width)
-                product_ref[parity, 0] = jnp.dot(
-                    left, spread_ref[jj, :, columns], preferred_element_type=jnp.float32
+                for part in range(2):
+                    product_ref[parity, part] = jnp.dot(
+                        parts[part], spread_ref[:, columns], preferred_element_type=jnp.float32
+                    )
+                weights = jnp.concatenate(
+                    [
+                        jnp.concatenate([held_ref[b, i, 2 * t + half, jj, part] for half in range(2)], axis=1)
+                        for part in range(2)
+                        for i in range(panels // TILE)
+                    ],
+                    axis=0,
                 )
-                product_ref[parity, 1] = jnp.dot(
-                    left, spread_ref[4 + jj, :, columns], preferred_element_type=jnp.float32
-                )
+                mono = jnp.dot(source, weights, preferred_element_type=jnp.float32)
                 for half in range(2):
                     inner = slice(half * LANES, (half + 1) * LANES)
                     lane_tile = t * 2 + half
                     lanes = slice(lane_tile * LANES, (lane_tile + 1) * LANES)
-                    sum_real = jnp.zeros((8, LANES), jnp.float32)
-                    sum_imag = jnp.zeros((8, LANES), jnp.float32)
+                    far_real = far_imag = near_real = near_imag = jnp.zeros((8, LANES), jnp.float32)
                     for p in range(panels // 8):
                         rows = slice(p * 8, p * 8 + 8)
                         inverse = inverse_ref[rows, lanes]
@@ -348,14 +354,17 @@
                         sine = sines[p % 2 * 8 : p % 2 * 8 + 8]
                         radial_real = product_ref[parity, 0, rows, inner] * inverse
                         radial_imag = product_ref[parity, 1, rows, inner] * inverse
-                        near = inverse * inverse_wave
-                        source_real = near * radial_real - (mono_imag[rows] + radial_imag)
-                        source_imag = near * radial_imag + (mono_real[rows] + radial_real)
-                        sum_real = sum_real + (cosine * source_real + sine * source_imag)
-                        sum_imag = sum_imag + (cosine * source_imag - sine * source_real)
+                        term_real = cosine * radial_real + sine * radial_imag
+                        term_imag = cosine * radial_imag - sine * radial_real
+                        far_real = far_real + term_real
+                        far_imag = far_imag + term_imag
+                        near_real = near_real + inverse * term_real
+                        near_imag = near_imag + inverse * term_imag
                     row = t * 4 + jj
-                    field_ref[b, 0, row : row + 1, inner] = jnp.sum(sum_real, axis=0, keepdims=True)
-                    field_ref[b, 1, row : row + 1, inner] = jnp.sum(sum_imag, axis=0, keepdims=True)
+                    sum_real = jnp.sum(near_real * inverse_wave - far_imag, axis=0, keepdims=True)
+                    sum_imag = jnp.sum(near_imag * inverse_wave + far_real, axis=0, keepdims=True)
+                    field_ref[b, 0, row : row + 1, inner] = sum_real + (mono[0:1, inner] + mono[2:3, inner])
+                    field_ref[b, 1, row : row + 1, inner] = sum_imag + (mono[1:2, inner] + mono[3:4, inner])
         return carry
 
     lax.fori_loop(0, BLOCKS, one_block, 0)
@@ -370,22 +379,22 @@
     panels, count = LANES, observers.shape[1]
     return pl.pallas_call(
         radiate_kernel,
-        in_specs=[SMEM, VMEM, VMEM, HBM, HBM, VMEM, VMEM],
+        in_specs=[SMEM, pl.BlockSpec(memory_space=pl.ANY), VMEM, HBM, HBM, VMEM, VMEM, VMEM],
         out_specs=VMEM,
         out_shape=jax.ShapeDtypeStruct((count // 4, 2, LANES), jnp.float32),
         scratch_shapes=[
             pltpu.VMEM((BLOCKS, panels, LANES), jnp.bfloat16),
-            pltpu.VMEM((BLOCKS, panels, LANES), jnp.float32),
             pltpu.VMEM((2, 2, panels, 256), jnp.float32),
             pltpu.VMEM((BLOCKS, 2, 16, 256), jnp.float32),
             pltpu.VMEM((panels, count), jnp.float32),
-            pltpu.VMEM((8, LANES, count), jnp.bfloat16),
-            pltpu.VMEM((1024, 1024), jnp.bfloat16),
+            pltpu.VMEM((LANES, count), jnp.bfloat16),
             pltpu.VMEM((2 * NF, CHANNELS * TIME), jnp.bfloat16),
             pltpu.VMEM((CHANNELS * 2 * NF, CHANNELS * TIME), jnp.bfloat16),
+            pltpu.VMEM((CHANNELS * TIME, LANES), jnp.bfloat16),
+            pltpu.VMEM((NF, 16, 2 * LANES), jnp.bfloat16),
             pltpu.VMEM((BLOCKS, panels // TILE, count // LANES, 4, 2, TILE, LANES), jnp.bfloat16),
             pltpu.SemaphoreType.DMA((BLOCKS,)),
-            pltpu.SemaphoreType.DMA,
+            pltpu.SemaphoreType.DMA((2,)),
         ],
         cost_estimate=pl.CostEstimate(flops=20_000_000_000, bytes_accessed=40_000_000, transcendentals=0),
         compiler_params=pltpu.CompilerParams(vmem_limit_bytes=40 << 20),
@@ -424,9 +433,9 @@
 
 def local_field(data, place, panel_position, scale, observers, bins):
     prepared = prepare(bins, place, observers, panel_position)
-    waves, table, columns = prepared
+    waves, table, columns, position = prepared
     held = [pltpu.with_memory_space_constraint(v, pltpu.HBM) for v in (waves, table)]
-    return radiate(bins, data, observers, (*held, columns), scale)
+    return radiate(bins, data, observers, (*held, columns, position), scale)
 
 
 def shards(samples, panel_position, panel_area, panel_counts, obs_position, freq_bins):

time: 95.4 us -> 92.5 us (0.970)
  Pallas kernels: 38.6 us -> 35.7 us
    pallas_call x1, Pallas kernels: 18.2 us -> 15.3 us  [radiate(): pl.pallas_call(radiate_kernel, in_specs=[SMEM, pl.BlockSpec(memory_space=...]
  transfers between devices with their start and end apart: 4 -> 4, of which waited for: 1 -> 1; matrix products, arithmetic and copies ran while one was open for 3% -> 4% of each run, Pallas kernels for 19% -> 20%
where the time goes in v3:
time: 92.5 us; the launch traced here: 92.2 us
  Pallas kernels  35.7 us (39%)
  blocking collectives  21.8 us (24%)
  starting transfers between devices  19 us (21%)
  waiting for transfers between devices  10 us (11%)
  local copies, waits for them, and re-layouts  4.05 us (4%)
  other arithmetic  1.44 us (2%)
    all_to_all x1, blocking collectives, shards(): arrived = lax.all_to_all(partial, ('panel', 'obs'), 0, 0, tiled=True)  21.8 us
    pallas_call x1, Pallas kernels, prepare(): pl.pallas_call(prepare_kernel, in_specs=[SMEM, SMEM, VMEM, VMEM], out_spe...  16.2 us
    pallas_call x1, Pallas kernels, radiate(): pl.pallas_call(radiate_kernel, in_specs=[SMEM, pl.BlockSpec(memory_space=...  15.3 us
    all_to_all x1, starting transfers between devices, shards(): lax.all_to_all(arrange(samples), ('panel', 'obs'), 0, 0, tiled=True)  13.2 us
    all_to_all x1, waiting for transfers between devices, shards(): lax.all_to_all(arrange(samples), ('panel', 'obs'), 0, 0, tiled=True)  9.99 us
    ppermute x3, starting transfers between devices, all_observers(): lax.ppermute(local, 'obs', [((i + shift) % size, i) for i in range(size)])  5.88 us
    pallas_call x1, Pallas kernels, arrange(): pl.pallas_call(arrange_kernel, in_specs=[HBM], out_specs=VMEM, out_shape=...  2.33 us
    pallas_call x1, Pallas kernels, gather(): pl.pallas_call(gather_kernel, in_specs=[VMEM], out_specs=VMEM, out_shape=...  1.88 us
  transfers between devices with their start and end apart: 4, of which 1 were waited for; matrix products, arithmetic and copies ran while one was open for 4% of the time, Pallas kernels for 20%

profile of v3, /device:TPU:1, one launch (start us, length us, event | category | flops | bytes accessed | tf_op | source)
XLA Modules:
  0.0 92.2 jit_solution(17674221554094040358)
XLA Ops:
  0.0 0.8 reshape.16
  0.8 0.1 copy.15
  0.9 2.2 %collective-permute-start.2 = (f32[12,64]{1,0:T(8,128)S(1)}, f32[12,64]{1,0:T(8,128)S(1)}, u32[]{:S(2)}, u32[]{:S(2)}) collective-permute-start(f32[12,64]{1,0:T(8,128)S(1)} %reshape.17), channel_id=1, source_target_pairs={{3,0},{0,1},{1,2},{2,3},{7,4},{4,5},{5,6},{6,7},{11,8},{8,9},{9,10... | collective-permute-start | bytes 9224 | tf_op jit(solution)/shard_map/ppermute | solution.py:427
  3.1 2.6 %collective-permute-start.1 = (f32[12,64]{1,0:T(8,128)S(1)}, f32[12,64]{1,0:T(8,128)S(1)}, u32[]{:S(2)}, u32[]{:S(2)}) collective-permute-start(f32[12,64]{1,0:T(8,128)S(1)} %reshape.17), channel_id=1, source_target_pairs={{2,0},{3,1},{0,2},{1,3},{6,4},{7,5},{4,6},{5,7},{10,8},{11,9},{8,1... | collective-permute-start | bytes 9224 | tf_op jit(solution)/shard_map/ppermute | solution.py:427
  5.7 1.1 %collective-permute-start = (f32[12,64]{1,0:T(8,128)S(1)}, f32[12,64]{1,0:T(8,128)S(1)}, u32[]{:S(2)}, u32[]{:S(2)}) collective-permute-start(f32[12,64]{1,0:T(8,128)S(1)} %reshape.17), channel_id=1, source_target_pairs={{1,0},{2,1},{3,2},{0,3},{5,4},{6,5},{7,6},{4,7},{9,8},{10,9},{11,1... | collective-permute-start | bytes 9224 | tf_op jit(solution)/shard_map/ppermute | solution.py:427
  6.8 2.3 %arrange.1 = bf16[256,4,4,128]{3,2,1,0:T(4,128)(2,1)} custom-call(bf16[4,4,32768]{2,1,0:T(4,128)(2,1)} %x_ref.1), custom_call_target="tpu_custom_call" | custom-call | tf_op jit(solution)/shard_map/arrange/pallas_call | solution.py:73
  9.1 13.2 %all-to-all-start = ((bf16[256,4,4,128]{3,2,1,0:T(4,128)(2,1)}), bf16[256,4,4,128]{3,2,1,0:T(4,128)(2,1)S(1)}, u32[]{:S(2)}, u32[]{:S(2)}) async-start(bf16[256,4,4,128]{3,2,1,0:T(4,128)(2,1)} %arrange.1), calls=%async_computation | async-start | bytes 2097152 | tf_op jit(solution)/shard_map/all_to_all | solution.py:442
  22.3 1.3 %dynamic_slice.10 = s32[1]{0:T(128)} dynamic-slice(s32[4]{0:T(128)} %param.9, s32[]{:T(128)S(6)} %select_n.22), dynamic_slice_sizes={1} | dynamic-slice | bytes 12 | tf_op jit(solution)/shard_map/dynamic_slice | solution.py:448
  23.6 1.4 %fusion.scale_ref = f32[1,128]{1,0:T(1,128)S(1)} fusion(f32[512]{0:T(512)} %param.8, s32[]{:T(128)S(6)} %select_n.23, s32[]{:T(128)} %bitcast.7), kind=kLoop, calls=%fused_computation.10 | loop fusion | flops 384 | bytes 1032 | tf_op jit(solution)/shard_map/broadcast_in_dim | solution.py:450
  25.1 0.0 collective-permute-done
  25.1 0.0 collective-permute-done.1
  25.1 0.0 collective-permute-done.2
  25.2 0.2 copy.17
  25.4 0.2 reshape.18.obs_ref
  25.6 0.0 copy-start
  25.6 0.7 copy-done
  26.3 0.0 copy-start.1
  26.3 0.7 copy-done.1
  27.0 0.0 copy-start.2
  27.0 16.2 %prepare.1 = (bf16[4,8,32,2,32,128]{5,4,3,2,1,0:T(8,128)(2,1)}, bf16[64,4096]{1,0:T(8,128)(2,1)}, f32[128,8]{1,0:T(8,128)S(1)}, f32[8,128]{1,0:T(8,128)S(1)}) custom-call(s32[32]{0:T(128)S(1)} %copy-done.1, s32[1]{0:T(128)} %bitcast.6.place_smem, f32[3,1024]{1,0:T(4,128)S(1)} %reshape.18.obs_ref, f32[3,512]{1,0:T(4,128)S(1)} %copy-done), custom_call_target="tpu_custom_call" | custom-call | flops 20000000000 | bytes 40000000 | tf_op jit(solution)/shard_map/prepare/pallas_call | solution.py:199
  43.2 10.0 %all-to-all-done = bf16[256,4,4,128]{3,2,1,0:T(4,128)(2,1)S(1)} async-done(((bf16[256,4,4,128]{3,2,1,0:T(4,128)(2,1)}), bf16[256,4,4,128]{3,2,1,0:T(4,128)(2,1)S(1)}, u32[]{:S(2)}, u32[]{:S(2)}) %all-to-all-start) | async-done | bytes 1048608 | tf_op jit(solution)/shard_map/all_to_all | solution.py:442
  53.1 0.0 copy-done.2
  53.1 15.3 %radiate.1 = f32[256,2,128]{2,1,0:T(2,128)S(1)} custom-call(s32[32]{0:T(128)S(1)} %copy-done.2, bf16[4096,128]{1,0:T(8,128)(2,1)S(1)} %bitcast.18, f32[3,1024]{1,0:T(4,128)S(1)} %reshape.18.obs_ref, bf16[4,8,32,2,32,128]{5,4,3,2,1,0:T(8,128)(2,1)} %get-tuple-element.9.waves_ref, bf16[64,4096]{1,0:T(8,128)(2,1)} %get-tuple-element.10.table_in_ref, ...), custom_call_target="tpu_custom_call" | custom-call | flops 20000000000 | bytes 40000000 | tf_op jit(solution)/shard_map/radiate/pallas_call | solution.py:380
  68.5 21.8 %all_to_all.10.x_ref = f32[256,2,128]{2,1,0:T(2,128)} all-to-all(f32[256,2,128]{2,1,0:T(2,128)S(1)} %radiate.1), channel_id=1, replica_groups=mesh['panel'=64,'obs'=4] {'panel','obs'}, dimensions={0} | all-to-all | bytes 524288 | tf_op jit(solution)/shard_map/all_to_all | solution.py:453
  90.3 1.9 %gather.1 = f32[2,4,32]{2,1,0:T(4,128)} custom-call(f32[256,2,128]{2,1,0:T(2,128)} %all_to_all.10.x_ref), custom_call_target="tpu_custom_call" | custom-call | tf_op jit(solution)/shard_map/gather/pallas_call | solution.py:413
  (11 shorter events, 0.1 us)
Async XLA Ops:
  0.9 24.2 %collective-permute-start.2 = (f32[12,64]{1,0:T(8,128)S(1)}, f32[12,64]{1,0:T(8,128)S(1)}, u32[]{:S(2)}, u32[]{:S(2)}) collective-permute-start(f32[12,64]{1,0:T(8,128)S(1)} %reshape.17), channel_id=1, source_target_pairs={{3,0},{0,1},{1,2},{2,3},{7,4},{4,5},{5,6},{6,7},{11,8},{8,9},{9,10... | collective-permute-start | bytes 9224 | tf_op jit(solution)/shard_map/ppermute | solution.py:427
  3.1 22.0 %collective-permute-start.1 = (f32[12,64]{1,0:T(8,128)S(1)}, f32[12,64]{1,0:T(8,128)S(1)}, u32[]{:S(2)}, u32[]{:S(2)}) collective-permute-start(f32[12,64]{1,0:T(8,128)S(1)} %reshape.17), channel_id=1, source_target_pairs={{2,0},{3,1},{0,2},{1,3},{6,4},{7,5},{4,6},{5,7},{10,8},{11,9},{8,1... | collective-permute-start | bytes 9224 | tf_op jit(solution)/shard_map/ppermute | solution.py:427
  5.7 19.4 %collective-permute-start = (f32[12,64]{1,0:T(8,128)S(1)}, f32[12,64]{1,0:T(8,128)S(1)}, u32[]{:S(2)}, u32[]{:S(2)}) collective-permute-start(f32[12,64]{1,0:T(8,128)S(1)} %reshape.17), channel_id=1, source_target_pairs={{1,0},{2,1},{3,2},{0,3},{5,4},{6,5},{7,6},{4,7},{9,8},{10,9},{11,1... | collective-permute-start | bytes 9224 | tf_op jit(solution)/shard_map/ppermute | solution.py:427
  9.1 44.0 %all-to-all-start = ((bf16[256,4,4,128]{3,2,1,0:T(4,128)(2,1)}), bf16[256,4,4,128]{3,2,1,0:T(4,128)(2,1)S(1)}, u32[]{:S(2)}, u32[]{:S(2)}) async-start(bf16[256,4,4,128]{3,2,1,0:T(4,128)(2,1)} %arrange.1), calls=%async_computation | async-start | bytes 2097152 | tf_op jit(solution)/shard_map/all_to_all | solution.py:442
  25.6 0.7 copy-start
  26.3 0.7 copy-start.1
  27.0 26.2 %copy-start.2 = (s32[32]{0:T(128)S(1)}, s32[32]{0:T(128)}, u32[]{:S(2)}) copy-start(s32[32]{0:T(128)} %bins_smem.3) | copy-start | bytes 388

commit v4 on v3

--- a/solution.py
+++ b/solution.py
@@ -51,7 +51,7 @@
     return part * horner(square, SIN_COEFFS), horner(square, COS_COEFFS)
 
 
-def arrange_kernel(x_ref, o_ref, held_ref, sem):
+def arrange_kernel(x_ref, o_ref, held_ref, made_ref, sem, out_sem):
     pieces, steps, _, piece = held_ref.shape
     copies = [
         pltpu.make_async_copy(x_ref.at[:, :, i * piece : (i + 1) * piece], held_ref.at[i], sem.at[i])
@@ -60,11 +60,19 @@
     for copy in copies:
         copy.start()
     blocks = piece // LANES
+
+    def outward(i):
+        done = pl.ds(i * blocks, blocks)
+        return pltpu.make_async_copy(made_ref.at[done], o_ref.at[done], out_sem.at[i])
+
     for i, copy in enumerate(copies):
         copy.wait()
         for block in range(blocks):
             for step in range(steps):
-                o_ref[i * blocks + block, step] = held_ref[i, step, :, block * LANES : (block + 1) * LANES]
+                made_ref[i * blocks + block, step] = held_ref[i, step, :, block * LANES : (block + 1) * LANES]
+        outward(i).start()
+    for i in range(pieces):
+        outward(i).wait()
 
 
 def arrange(samples):
@@ -73,10 +81,12 @@
     return pl.pallas_call(
         arrange_kernel,
         in_specs=[HBM],
-        out_specs=VMEM,
-        out_shape=jax.ShapeDtypeStruct((panels // LANES, steps, channels, LANES), samples.dtype),
+        out_specs=HBM,
+        out_shape=pltpu.HBM((panels // LANES, steps, channels, LANES), samples.dtype),
         scratch_shapes=[
             pltpu.VMEM((pieces, steps, channels, panels // pieces), samples.dtype),
+            pltpu.VMEM((panels // LANES, steps, channels, LANES), samples.dtype),
+            pltpu.SemaphoreType.DMA((pieces,)),
             pltpu.SemaphoreType.DMA((pieces,)),
         ],
         compiler_params=pltpu.CompilerParams(vmem_limit_bytes=8 << 20),
@@ -227,12 +237,12 @@
 def radiate_kernel(
     bins_smem,
     data_in_ref,
-    obs_ref,
+    obs_in_ref,
     waves_ref,
     table_in_ref,
-    column_ref,
-    position_ref,
-    scale_ref,
+    column_in_ref,
+    position_in_ref,
+    scale_in_ref,
     o_ref,
     left_ref,
     product_ref,
@@ -244,9 +254,28 @@
     data_ref,
     source_ref,
     held_ref,
+    obs_ref,
+    column_ref,
+    position_ref,
+    scale_ref,
+    made_ref,
     sem,
     in_sem,
+    out_sem,
 ):
+    small = [
+        pltpu.make_async_copy(source, target, in_sem.at[2 + i])
+        for i, (source, target) in enumerate(
+            (
+                (obs_in_ref, obs_ref),
+                (column_in_ref, column_ref),
+                (position_in_ref, position_ref),
+                (scale_in_ref, scale_ref),
+            )
+        )
+    ]
+    for copy in small:
+        copy.start()
     table_copy = pltpu.make_async_copy(table_in_ref, narrow_ref, in_sem.at[0])
     table_copy.start()
     data_copy = pltpu.make_async_copy(data_in_ref, data_ref, in_sem.at[1])
@@ -254,6 +283,9 @@
     for b in range(AHEAD):
         wave_fetch(waves_ref, held_ref, sem, b).start()
     rows = 2 * NF
+
+    for copy in small:
+        copy.wait()
 
     obs = obs_ref[...]
     high = obs.astype(jnp.bfloat16).astype(jnp.float32)
@@ -368,20 +400,29 @@
         return carry
 
     lax.fori_loop(0, BLOCKS, one_block, 0)
-    for part in range(2):
-        flat = jnp.concatenate(
-            [field_ref[b, part, 4 * t : 4 * t + 4] for t in range(4) for b in range(BLOCKS)], axis=0
-        )
-        o_ref[:, part, :] = flat.T
+    copies = []
+    for half in range(2):
+        lanes = slice(half * LANES, (half + 1) * LANES)
+        for part in range(2):
+            flat = jnp.concatenate(
+                [field_ref[b, part, 4 * t : 4 * t + 4, lanes] for t in range(4) for b in range(BLOCKS)], axis=0
+            )
+            made_ref[pl.ds(half * 2 * LANES + part, LANES, 2), :] = flat.T
+        done = pl.ds(half * 2 * LANES, 2 * LANES)
+        copies.append(pltpu.make_async_copy(made_ref.at[done], o_ref.at[done], out_sem.at[half]))
+        copies[half].start()
+    for copy in copies:
+        copy.wait()
 
 
 def radiate(bins, data, observers, prepared, scale):
     panels, count = LANES, observers.shape[1]
+    anywhere = pl.BlockSpec(memory_space=pl.ANY)
     return pl.pallas_call(
         radiate_kernel,
-        in_specs=[SMEM, pl.BlockSpec(memory_space=pl.ANY), VMEM, HBM, HBM, VMEM, VMEM, VMEM],
-        out_specs=VMEM,
-        out_shape=jax.ShapeDtypeStruct((count // 4, 2, LANES), jnp.float32),
+        in_specs=[SMEM, anywhere, anywhere, HBM, HBM, anywhere, anywhere, anywhere],
+        out_specs=HBM,
+        out_shape=pltpu.HBM((count // 2, LANES), jnp.float32),
         scratch_shapes=[
             pltpu.VMEM((BLOCKS, panels, LANES), jnp.bfloat16),
             pltpu.VMEM((2, 2, panels, 256), jnp.float32),
@@ -393,7 +434,13 @@
             pltpu.VMEM((CHANNELS * TIME, LANES), jnp.bfloat16),
             pltpu.VMEM((NF, 16, 2 * LANES), jnp.bfloat16),
             pltpu.VMEM((BLOCKS, panels // TILE, count // LANES, 4, 2, TILE, LANES), jnp.bfloat16),
+            pltpu.VMEM((3, count), jnp.float32),
+            pltpu.VMEM((panels, 8), jnp.float32),
+            pltpu.VMEM((8, panels), jnp.float32),
+            pltpu.VMEM((1, panels), jnp.float32),
+            pltpu.VMEM((count // 2, LANES), jnp.float32),
             pltpu.SemaphoreType.DMA((BLOCKS,)),
+            pltpu.SemaphoreType.DMA((6,)),
             pltpu.SemaphoreType.DMA((2,)),
         ],
         cost_estimate=pl.CostEstimate(flops=20_000_000_000, bytes_accessed=40_000_000, transcendentals=0),
@@ -403,10 +450,17 @@
 
 
 def gather_kernel(x_ref, o_ref):
-    total = jnp.sum(x_ref[...], axis=0)
+    total = jnp.zeros((8, LANES), jnp.float32)
+    sums = [total, total, total, total]
+    for i in range(x_ref.shape[0] // 8):
+        sums[i % 4] = sums[i % 4] + x_ref[8 * i : 8 * i + 8, :]
+    total = (sums[0] + sums[1]) + (sums[2] + sums[3])
     for part in range(2):
+        whole = (total[part : part + 1] + total[part + 2 : part + 3]) + (
+            total[part + 4 : part + 5] + total[part + 6 : part + 7]
+        )
         for i in range(4):
-            o_ref[part, i : i + 1, :] = total[part : part + 1, i * NF : (i + 1) * NF]
+            o_ref[part, i : i + 1, :] = whole[:, i * NF : (i + 1) * NF]
 
 
 def gather(arrived):
@@ -450,7 +504,9 @@
     scale = jnp.where(lane_ids < count, area * (1.0 / (4.0 * math.pi)), 0.0)[None, :]
 
     partial = local_field(data, place.reshape(1), panel_position, scale, observers, freq_bins)
+    partial = partial.reshape(-1, 2, LANES)
     arrived = lax.all_to_all(partial, ("panel", "obs"), 0, 0, tiled=True)
+    arrived = arrived.reshape(-1, LANES)
     return jnp.transpose(gather(arrived), (0, 2, 1))
 
 

time: 92.5 us -> 93 us (level)
  transfers between devices with their start and end apart: 4 -> 4, of which waited for: 1 -> 1; matrix products, arithmetic and copies ran while one was open for 4% -> 3% of each run, Pallas kernels for 20% -> 20%
where the time goes in v4:
time: 93 us; the launch traced here: 92.6 us
  Pallas kernels  35.9 us (39%)
  blocking collectives  22 us (24%)
  starting transfers between devices  19 us (20%)
  waiting for transfers between devices  10 us (11%)
  local copies, waits for them, and re-layouts  4.05 us (4%)
  other arithmetic  1.44 us (2%)
    all_to_all x1, blocking collectives, shards(): arrived = lax.all_to_all(partial, ('panel', 'obs'), 0, 0, tiled=True)  22 us
    pallas_call x1, Pallas kernels, prepare(): pl.pallas_call(prepare_kernel, in_specs=[SMEM, SMEM, VMEM, VMEM], out_spe...  16.2 us
    pallas_call x1, Pallas kernels, radiate(): pl.pallas_call(radiate_kernel, in_specs=[SMEM, anywhere, anywhere, HBM, H...  16.1 us
    all_to_all x1, starting transfers between devices, shards(): lax.all_to_all(arrange(samples), ('panel', 'obs'), 0, 0, tiled=True)  13.2 us
    all_to_all x1, waiting for transfers between devices, shards(): lax.all_to_all(arrange(samples), ('panel', 'obs'), 0, 0, tiled=True)  9.99 us
    ppermute x3, starting transfers between devices, all_observers(): lax.ppermute(local, 'obs', [((i + shift) % size, i) for i in range(size)])  5.88 us
    pallas_call x1, Pallas kernels, arrange(): pl.pallas_call(arrange_kernel, in_specs=[HBM], out_specs=HBM, out_shape=p...  2.09 us
  transfers between devices with their start and end apart: 4, of which 1 were waited for; matrix products, arithmetic and copies ran while one was open for 3% of the time, Pallas kernels for 20%

profile of v4, /device:TPU:1, one launch (start us, length us, event | category | flops | bytes accessed | tf_op | source)
XLA Modules:
  0.0 92.6 jit_solution(8781183954376611954)
XLA Ops:
  0.0 0.8 reshape.22
  0.8 0.1 copy.15
  0.9 2.2 %collective-permute-start.2 = (f32[12,64]{1,0:T(8,128)S(1)}, f32[12,64]{1,0:T(8,128)S(1)}, u32[]{:S(2)}, u32[]{:S(2)}) collective-permute-start(f32[12,64]{1,0:T(8,128)S(1)} %reshape.23), channel_id=1, source_target_pairs={{3,0},{0,1},{1,2},{2,3},{7,4},{4,5},{5,6},{6,7},{11,8},{8,9},{9,10... | collective-permute-start | bytes 9224 | tf_op jit(solution)/shard_map/ppermute | solution.py:481
  3.1 2.6 %collective-permute-start.1 = (f32[12,64]{1,0:T(8,128)S(1)}, f32[12,64]{1,0:T(8,128)S(1)}, u32[]{:S(2)}, u32[]{:S(2)}) collective-permute-start(f32[12,64]{1,0:T(8,128)S(1)} %reshape.23), channel_id=1, source_target_pairs={{2,0},{3,1},{0,2},{1,3},{6,4},{7,5},{4,6},{5,7},{10,8},{11,9},{8,1... | collective-permute-start | bytes 9224 | tf_op jit(solution)/shard_map/ppermute | solution.py:481
  5.7 1.1 %collective-permute-start = (f32[12,64]{1,0:T(8,128)S(1)}, f32[12,64]{1,0:T(8,128)S(1)}, u32[]{:S(2)}, u32[]{:S(2)}) collective-permute-start(f32[12,64]{1,0:T(8,128)S(1)} %reshape.23), channel_id=1, source_target_pairs={{1,0},{2,1},{3,2},{0,3},{5,4},{6,5},{7,6},{4,7},{9,8},{10,9},{11,1... | collective-permute-start | bytes 9224 | tf_op jit(solution)/shard_map/ppermute | solution.py:481
  6.8 2.1 %arrange.1 = bf16[256,4,4,128]{3,2,1,0:T(4,128)(2,1)} custom-call(bf16[4,4,32768]{2,1,0:T(4,128)(2,1)} %x_ref.1), custom_call_target="tpu_custom_call" | custom-call | tf_op jit(solution)/shard_map/arrange/pallas_call | solution.py:81
  8.9 13.2 %all-to-all-start = ((bf16[256,4,4,128]{3,2,1,0:T(4,128)(2,1)}), bf16[256,4,4,128]{3,2,1,0:T(4,128)(2,1)S(1)}, u32[]{:S(2)}, u32[]{:S(2)}) async-start(bf16[256,4,4,128]{3,2,1,0:T(4,128)(2,1)} %arrange.1), calls=%async_computation | async-start | bytes 2097152 | tf_op jit(solution)/shard_map/all_to_all | solution.py:496
  22.1 1.3 %dynamic_slice.10 = s32[1]{0:T(128)} dynamic-slice(s32[4]{0:T(128)} %param.9, s32[]{:T(128)S(6)} %select_n.22), dynamic_slice_sizes={1} | dynamic-slice | bytes 12 | tf_op jit(solution)/shard_map/dynamic_slice | solution.py:502
  23.4 1.4 %fusion.scale_in_ref = f32[1,128]{1,0:T(1,128)S(1)} fusion(f32[512]{0:T(512)} %param.8, s32[]{:T(128)S(6)} %select_n.23, s32[]{:T(128)} %bitcast.7), kind=kLoop, calls=%fused_computation.10 | loop fusion | flops 384 | bytes 1032 | tf_op jit(solution)/shard_map/broadcast_in_dim | solution.py:504
  24.8 0.0 collective-permute-done
  24.8 0.0 collective-permute-done.1
  24.9 0.0 collective-permute-done.2
  24.9 0.2 copy.17
  25.1 0.2 reshape.24.obs_ref.obs_in_ref
  25.4 0.0 copy-start
  25.4 0.7 copy-done
  26.1 0.0 copy-start.1
  26.1 0.7 copy-done.1
  26.8 0.0 copy-start.2
  26.8 16.2 %prepare.1 = (bf16[4,8,32,2,32,128]{5,4,3,2,1,0:T(8,128)(2,1)}, bf16[64,4096]{1,0:T(8,128)(2,1)}, f32[128,8]{1,0:T(8,128)S(1)}, f32[8,128]{1,0:T(8,128)S(1)}) custom-call(s32[32]{0:T(128)S(1)} %copy-done.1, s32[1]{0:T(128)} %bitcast.6.place_smem, f32[3,1024]{1,0:T(4,128)S(1)} %reshape.24.obs_ref.obs_in_ref, f32[3,512]{1,0:T(4,128)S(1)} %copy-done), custom_call_target="tpu_custom_call" | custom-call | flops 20000000000 | bytes 40000000 | tf_op jit(solution)/shard_map/prepare/pallas_call | solution.py:209
  42.9 10.0 %all-to-all-done = bf16[256,4,4,128]{3,2,1,0:T(4,128)(2,1)S(1)} async-done(((bf16[256,4,4,128]{3,2,1,0:T(4,128)(2,1)}), bf16[256,4,4,128]{3,2,1,0:T(4,128)(2,1)S(1)}, u32[]{:S(2)}, u32[]{:S(2)}) %all-to-all-start) | async-done | bytes 1048608 | tf_op jit(solution)/shard_map/all_to_all | solution.py:496
  52.9 0.0 copy-done.2
  52.9 16.1 %radiate.1 = f32[512,128]{1,0:T(8,128)} custom-call(s32[32]{0:T(128)S(1)} %copy-done.2, bf16[4096,128]{1,0:T(8,128)(2,1)S(1)} %bitcast.20, f32[3,1024]{1,0:T(4,128)S(1)} %reshape.24.obs_ref.obs_in_ref, bf16[4,8,32,2,32,128]{5,4,3,2,1,0:T(8,128)(2,1)} %get-tuple-element.9.waves_ref, bf16[64,4096]{1,0:T(8,128)(2,1)} %get-tuple-element.10.table_in_ref, ...), custom_call_target="tpu_custom_call" | custom-call | flops 20000000000 | bytes 40000000 | tf_op jit(solution)/shard_map/radiate/pallas_call | solution.py:421
  69.0 22.0 %all_to_all.10 = f32[256,2,128]{2,1,0:T(2,128)} all-to-all(f32[256,2,128]{2,1,0:T(2,128)} %bitcast.23), channel_id=1, replica_groups=mesh['panel'=64,'obs'=4] {'panel','obs'}, dimensions={0} | all-to-all | bytes 524288 | tf_op jit(solution)/shard_map/all_to_all | solution.py:508
  91.0 1.6 %gather.1 = f32[2,4,32]{2,1,0:T(4,128)} custom-call(f32[512,128]{1,0:T(8,128)} %bitcast.21), custom_call_target="tpu_custom_call" | custom-call | tf_op jit(solution)/shard_map/gather/pallas_call | solution.py:467
  (11 shorter events, 0.1 us)
Async XLA Ops:
  0.9 24.0 %collective-permute-start.2 = (f32[12,64]{1,0:T(8,128)S(1)}, f32[12,64]{1,0:T(8,128)S(1)}, u32[]{:S(2)}, u32[]{:S(2)}) collective-permute-start(f32[12,64]{1,0:T(8,128)S(1)} %reshape.23), channel_id=1, source_target_pairs={{3,0},{0,1},{1,2},{2,3},{7,4},{4,5},{5,6},{6,7},{11,8},{8,9},{9,10... | collective-permute-start | bytes 9224 | tf_op jit(solution)/shard_map/ppermute | solution.py:481
  3.1 21.7 %collective-permute-start.1 = (f32[12,64]{1,0:T(8,128)S(1)}, f32[12,64]{1,0:T(8,128)S(1)}, u32[]{:S(2)}, u32[]{:S(2)}) collective-permute-start(f32[12,64]{1,0:T(8,128)S(1)} %reshape.23), channel_id=1, source_target_pairs={{2,0},{3,1},{0,2},{1,3},{6,4},{7,5},{4,6},{5,7},{10,8},{11,9},{8,1... | collective-permute-start | bytes 9224 | tf_op jit(solution)/shard_map/ppermute | solution.py:481
  5.7 19.1 %collective-permute-start = (f32[12,64]{1,0:T(8,128)S(1)}, f32[12,64]{1,0:T(8,128)S(1)}, u32[]{:S(2)}, u32[]{:S(2)}) collective-permute-start(f32[12,64]{1,0:T(8,128)S(1)} %reshape.23), channel_id=1, source_target_pairs={{1,0},{2,1},{3,2},{0,3},{5,4},{6,5},{7,6},{4,7},{9,8},{10,9},{11,1... | collective-permute-start | bytes 9224 | tf_op jit(solution)/shard_map/ppermute | solution.py:481
  8.9 44.0 %all-to-all-start = ((bf16[256,4,4,128]{3,2,1,0:T(4,128)(2,1)}), bf16[256,4,4,128]{3,2,1,0:T(4,128)(2,1)S(1)}, u32[]{:S(2)}, u32[]{:S(2)}) async-start(bf16[256,4,4,128]{3,2,1,0:T(4,128)(2,1)} %arrange.1), calls=%async_computation | async-start | bytes 2097152 | tf_op jit(solution)/shard_map/all_to_all | solution.py:496
  25.4 0.7 copy-start
  26.1 0.7 copy-start.1
  26.8 26.2 %copy-start.2 = (s32[32]{0:T(128)S(1)}, s32[32]{0:T(128)}, u32[]{:S(2)}) copy-start(s32[32]{0:T(128)} %bins_smem.3) | copy-start | bytes 388
